TPU v7x, 32 devices: a whole 2x2x4 slice. The times are simulated.
32 devices in a mesh: seq: 16 (over z, y, x), head: 2 (over core).
Axes of the slice: x: 2, y: 2, z: 4, core: 2. Of those that a mesh axis runs over, the one named last changes fastest.
Arguments:
- tokens: bfloat16 [8192, 3584], P('seq', 'head'), may hold values from -6 to 6
- pre_gain: float32 [3584], replicated, may hold values from 0.5 to 1.5
- query_weight: bfloat16 [3584, 2048], P(None, 'head'), may hold values from -0.375 to 0.375
- key_weight: bfloat16 [3584, 1024], P(None, 'head'), may hold values from -0.375 to 0.375
- value_weight: bfloat16 [3584, 1024], P(None, 'head'), may hold values from -0.09375 to 0.09375
- out_weight: bfloat16 [2048, 3584], P('head'), may hold values from -0.5 to 0.5
- post_gain: float32 [3584], P('head'), may hold values from 0.5 to 1.5
Outputs:
- layer_out: bfloat16 [8192, 3584], P('seq', 'head')
All inputs are finite; a program needn't handle non-finite values.
Results may differ from a plain program's by a relative error of at most 0.013.
The roundings to bfloat16 on the way count: a program that leaves them out, or rounds other values in their place, can miss the bound.
Values may be sent and summed in bfloat16 or wider, within the bound.
A program may use at most 192 MiB of HBM per device.

v0:
```python
import functools
import math

import jax
import jax.numpy as jnp
from jax import lax
from jax.experimental import pallas as pl
from jax.experimental.pallas import tpu as pltpu
from jax.sharding import PartitionSpec as P

HD = 256
WINDOW = 4096

softcap_limit = 50.0
rope_base = 10000.0
norm_epsilon = 1e-06

ROW_TILE = 512

PIECES = 2
X_KV, X_Q, X_OUT, Z_NEAR, Z_FAR, Y_NEAR, Y_FAR, MESSAGES = 0, 2, 3, 5, 9, 13, 17, 21


def attention_kernel(
    blocks, rows, normed_ref, weight_ref, cosine_ref, sine_ref, kv_ref, out_ref,
    held, queries, asked, total, mass, leaving, landed, send_sems, recv_sems,
):
    group = 2 * 2
    me = lax.axis_index("seq")
    x = me % 2
    y = (me // 2) % 2
    x_mate = me + 1 - 2 * x
    y_mate = me + 2 - 4 * y
    z_next = me + group
    has_next = z_next < blocks
    has_prev = me >= group
    has_far = me >= 2 * group
    first_row = y == 0
    second_row = y == 1

    def copy(message, src, dst, device):
        return pltpu.make_async_remote_copy(
            src_ref=src,
            dst_ref=dst,
            send_sem=send_sems.at[message],
            recv_sem=recv_sems.at[message],
            device_id={"seq": device},
            device_id_type=pl.DeviceIdType.MESH,
        )

    barrier = pltpu.get_barrier_semaphore()

    def greet(device):
        pl.semaphore_signal(
            barrier, inc=1, device_id={"seq": device}, device_id_type=pl.DeviceIdType.MESH
        )

    greet(x_mate)
    greet(y_mate)
    pl.when(has_next)(lambda: greet(z_next))
    pl.when(has_prev)(lambda: greet(me - group))
    pl.semaphore_wait(barrier, 2 + has_next.astype(jnp.int32) + has_prev.astype(jnp.int32))

    pieces = [(r, h) for r in range(2) for h in range(PIECES)]
    near = lambda r, h: kv_ref.at[x, h] if r == 0 else held.at[0, 1, h]

    def copies(base, source, slot, device):
        return {
            (r, h): copy(base + PIECES * r + h, source(r, h), held.at[slot, r, h], device)
            for r, h in pieces
        }

    arrived = lambda slot: lambda r, h: held.at[slot, r, h]
    send_kv = [
        copy(X_KV + h, kv_ref.at[1 - x, h], held.at[0, 1, h], x_mate) for h in range(PIECES)
    ]
    send_q = copy(X_Q, asked, queries.at[1], x_mate)
    z_near = copies(Z_NEAR, near, 2, z_next)
    z_far = copies(Z_FAR, arrived(2), 4, z_next)
    y_up_near = copies(Y_NEAR, near, 1, y_mate)
    y_up_far = copies(Y_FAR, arrived(2), 3, y_mate)
    y_down_near = copies(Y_NEAR, arrived(2), 1, y_mate)
    y_down_far = copies(Y_FAR, arrived(4), 3, y_mate)

    for h in range(PIECES):
        send_kv[h].start()
        pl.when(has_next)(lambda: z_near[0, h].start())
        pl.when(first_row)(lambda: y_up_near[0, h].start())

    tiles_per_side = 2 * rows // ROW_TILE
    tiles_per_head = rows // ROW_TILE

    def ask(whose, store):
        def tile(t, carry):
            head = t // tiles_per_head
            start = pl.multiple_of((t % tiles_per_head) * ROW_TILE, ROW_TILE)
            at = pl.multiple_of((2 * whose + head) * HD, HD)
            value = jnp.dot(
                normed_ref[pl.ds(start, ROW_TILE), :],
                weight_ref[:, pl.ds(at, HD)],
                preferred_element_type=jnp.float32,
            )
            store(
                head,
                pl.ds(start, ROW_TILE),
                rotated(
                    value,
                    cosine_ref[pl.ds(start, ROW_TILE), :],
                    sine_ref[pl.ds(start, ROW_TILE), :],
                ),
            )
            return carry

        lax.fori_loop(0, tiles_per_side, tile, 0)

    def store_asked(head, where, value):
        asked[head, where, :] = value

    def store_own(head, where, value):
        queries[0, head, where, :] = value

    ask(1 - x, store_asked)

    def pass_mate(h):
        send_kv[h].wait_recv()
        pl.when(has_next)(lambda: z_near[1, h].start())
        pl.when(first_row)(lambda: y_up_near[1, h].start())

    def pass_near(r, h):
        z_near[r, h].wait_recv()
        pl.when(has_next)(lambda: z_far[r, h].start())
        pl.when(first_row)(lambda: y_up_far[r, h].start())
        pl.when(second_row)(lambda: y_down_near[r, h].start())

    def pass_far(r, h):
        z_far[r, h].wait_recv()
        pl.when(second_row)(lambda: y_down_far[r, h].start())

    pass_mate(0)
    pl.when(has_prev)(lambda: pass_near(0, 0))
    send_q.start()
    ask(x, store_own)
    total[...] = jnp.zeros_like(total)
    mass[...] = jnp.zeros_like(mass)
    pass_mate(1)
    pl.when(has_prev)(lambda: pass_near(0, 1))

    inner = 1.0 / (math.sqrt(HD) * softcap_limit)
    outer = softcap_limit / math.log(2.0)

    def attend(block, first, last, distances):
        keys_here = rows // PIECES

        def tile(t, carry):
            side = t // tiles_per_side
            within = t % tiles_per_side
            head = within // tiles_per_head
            start = pl.multiple_of((within % tiles_per_head) * ROW_TILE, ROW_TILE)
            q = queries[side, head, pl.ds(start, ROW_TILE), :]
            part = None
            added = None
            for h in range(PIECES):
                scores = lax.dot_general(
                    q, block[h, 0], (((1,), (1,)), ((), ())), preferred_element_type=jnp.float32
                )
                weights = jnp.exp2(outer * jnp.tanh(scores * inner))
                if distances is not None:
                    distance = jnp.where(side == 0, distances[0], distances[1])
                    offset = (
                        distance * rows
                        + start
                        - h * keys_here
                        + lax.broadcasted_iota(jnp.int32, weights.shape, 0)
                        - lax.broadcasted_iota(jnp.int32, weights.shape, 1)
                    )
                    weights = jnp.where((offset >= 0) & (offset < WINDOW), weights, 0.0)
                for k in range(keys_here // 128):
                    lanes = weights[:, k * 128 : (k + 1) * 128]
                    part = lanes if part is None else part + lanes
                product = jnp.dot(
                    weights.astype(jnp.bfloat16), block[h, 1], preferred_element_type=jnp.float32
                )
                added = product if added is None else added + product
            mass[side, head, pl.ds(start, ROW_TILE), :] += part
            total[side, head, pl.ds(start, ROW_TILE), :] += added
            return carry

        lax.fori_loop(first, last, tile, 0)

    both = 2 * tiles_per_side
    reach = WINDOW // rows

    def ahead(d, r, side):
        if side == r:
            return jnp.int32(2 * d)
        return 2 * d + (2 * x - 1 if side == 0 else 1 - 2 * x)

    def edge(d, r):
        return (ahead(d, r, 0), ahead(d, r, 1))

    def bounds(d, r):
        low, high = edge(d, r)
        fits = lambda e: (e >= 0) & (e <= reach)
        first = jnp.where(fits(low), 0, tiles_per_side)
        last = jnp.where(fits(high), both, tiles_per_side)
        return first, last

    def whole(slot, r):
        attend(held.at[slot, r], 0, both, None)

    def arrive_near(r):
        for h in range(PIECES):
            y_up_near[r, h].wait_recv()
        whole(1, r)

    def arrive_far(r):
        for h in range(PIECES):
            y_up_far[r, h].wait_recv()
        whole(3, r)

    def farthest(r):
        first, last = bounds(4, r)
        attend(held.at[4, r], first, last, edge(4, r))

    attend(kv_ref.at[x], 0, tiles_per_side, edge(0, 0))
    pl.when(has_prev)(lambda: pass_near(1, 0))
    send_q.wait_recv()
    pl.when(has_prev)(lambda: pass_near(1, 1))
    attend(kv_ref.at[x], tiles_per_side, bounds(0, 0)[1], edge(0, 0))
    first, last = bounds(0, 1)
    attend(held.at[0, 1], first, last, edge(0, 1))
    pl.when(has_far)(lambda: pass_far(0, 0))
    pl.when(has_prev)(lambda: whole(2, 0))
    pl.when(has_far)(lambda: pass_far(0, 1))
    pl.when(has_prev)(lambda: whole(2, 1))
    pl.when(me >= 2)(lambda: arrive_near(0))
    pl.when(has_far)(lambda: pass_far(1, 0))
    pl.when(has_far)(lambda: farthest(0))
    pl.when(has_far)(lambda: pass_far(1, 1))
    pl.when(me >= 2)(lambda: arrive_near(1))
    pl.when(has_far)(lambda: farthest(1))
    pl.when(me >= 6)(lambda: arrive_far(0))
    pl.when(me >= 6)(lambda: arrive_far(1))

    def finished(side, head):
        weight = jnp.sum(mass[side, head], axis=-1, keepdims=True)
        return (total[side, head] / weight).astype(jnp.bfloat16)

    send_out = [copy(X_OUT + head, leaving.at[head], landed.at[head], x_mate) for head in range(2)]
    leaving[0] = finished(1, 0)
    leaving[1] = finished(1, 1)
    send_out[0].start()
    for head in range(2):
        at = pl.multiple_of((2 * x + head) * HD, HD)
        out_ref[:, pl.ds(at, HD)] = finished(0, head)
        if head == 0:
            send_out[1].start()
    for head in range(2):
        send_out[head].wait_recv()
        at = pl.multiple_of((2 * (1 - x) + head) * HD, HD)
        out_ref[:, pl.ds(at, HD)] = landed[head]

    send_q.wait_send()
    for h in range(PIECES):
        send_kv[h].wait_send()
        send_out[h].wait_send()
    for r, h in pieces:
        pl.when(has_next)(lambda: z_near[r, h].wait_send())
        pl.when(has_next & has_prev)(lambda: z_far[r, h].wait_send())
        pl.when(first_row)(lambda: y_up_near[r, h].wait_send())
        pl.when(first_row & has_prev)(lambda: y_up_far[r, h].wait_send())
        pl.when(second_row & has_prev)(lambda: y_down_near[r, h].wait_send())
        pl.when(second_row & has_far)(lambda: y_down_far[r, h].wait_send())


def attention(normed, weight, cosine, sine, kv, blocks):
    rows = normed.shape[0]
    half = (2, rows, HD)
    vmem = pl.BlockSpec(memory_space=pltpu.VMEM)
    return pl.pallas_call(
        functools.partial(attention_kernel, blocks, rows),
        out_shape=jax.ShapeDtypeStruct((rows, 4 * HD), jnp.bfloat16),
        in_specs=[vmem] * 5,
        out_specs=vmem,
        scratch_shapes=[
            pltpu.VMEM((5, 2) + kv.shape[1:], jnp.bfloat16),
            pltpu.VMEM((2,) + half, jnp.bfloat16),
            pltpu.VMEM(half, jnp.bfloat16),
            pltpu.VMEM((2,) + half, jnp.float32),
            pltpu.VMEM((2, 2, rows, 128), jnp.float32),
            pltpu.VMEM(half, jnp.bfloat16),
            pltpu.VMEM(half, jnp.bfloat16),
            pltpu.SemaphoreType.DMA((MESSAGES,)),
            pltpu.SemaphoreType.DMA((MESSAGES,)),
        ],
        compiler_params=pltpu.CompilerParams(
            collective_id=0, has_side_effects=True, vmem_limit_bytes=48 * 1024 * 1024
        ),
    )(normed, weight, cosine, sine, kv)


def norm_kernel(own_ref, other_ref, gain_ref, out_ref):
    side = lax.axis_index("head")
    width = own_ref.shape[1]
    lines = 16

    def chunk(i, carry):
        at_rows = pl.ds(pl.multiple_of(i * lines, lines), lines)
        squares = jnp.zeros((lines, 1), jnp.float32)
        for ref in (own_ref, other_ref):
            values = ref[at_rows, :].astype(jnp.float32)
            squares = squares + jnp.sum(values * values, axis=-1, keepdims=True)
        scale = lax.rsqrt(squares / (2 * width) + norm_epsilon)
        for ref, place in ((own_ref, side), (other_ref, 1 - side)):
            at = pl.ds(pl.multiple_of(place * width, width), width)
            values = ref[at_rows, :].astype(jnp.float32)
            out_ref[at_rows, at] = (values * scale * gain_ref[:, at]).astype(jnp.bfloat16)
        return carry

    lax.fori_loop(0, own_ref.shape[0] // lines, chunk, 0, unroll=2)


def norm(own, other, gain):
    rows, width = own.shape
    step = rows // 4
    return pl.pallas_call(
        norm_kernel,
        grid=(rows // step,),
        out_shape=jax.ShapeDtypeStruct((rows, 2 * width), jnp.bfloat16),
        in_specs=[
            pl.BlockSpec((step, width), lambda i: (i, 0)),
            pl.BlockSpec((step, width), lambda i: (i, 0)),
            pl.BlockSpec((1, 2 * width), lambda i: (0, 0)),
        ],
        out_specs=pl.BlockSpec((step, 2 * width), lambda i: (i, 0)),
    )(own, other, gain[None, :])


def swap_heads(shard):
    return lax.ppermute(shard, "head", [(0, 1), (1, 0)])


def rope_tables(positions):
    midpoint = HD // 2
    frequency = jnp.exp(
        -jnp.log(rope_base) * (2.0 * jnp.arange(midpoint, dtype=jnp.float32) / HD)
    )
    angles = positions.astype(jnp.float32)[:, None] * frequency[None, :]
    return jnp.cos(angles), jnp.sin(angles)


def rotated(head, cosine, sine):
    midpoint = HD // 2
    leading, trailing = head[:, :midpoint], head[:, midpoint:]
    return jnp.concatenate(
        [leading * cosine - trailing * sine, trailing * cosine + leading * sine], axis=-1
    ).astype(jnp.bfloat16)


def local(blocks, tokens, pre_gain, query_weight, key_weight, value_weight, out_weight, post_gain):
    rows, width = tokens.shape
    side = lax.axis_index("head")
    other = swap_heads(tokens)
    normed = norm(tokens, other, pre_gain)
    positions = lax.axis_index("seq") * rows + jnp.arange(rows, dtype=jnp.int32)
    cosine, sine = rope_tables(positions)
    project = lambda weight: jnp.dot(normed, weight, preferred_element_type=jnp.float32)
    k_all, v_all = project(key_weight), project(value_weight)
    head_of = lambda a, h: a[:, h * HD : (h + 1) * HD]
    in_pieces = lambda a: a.reshape(PIECES, rows // PIECES, HD)
    kv = jnp.stack(
        [
            jnp.stack(
                [
                    in_pieces(rotated(head_of(k_all, k), cosine, sine)),
                    in_pieces(head_of(v_all, k).astype(jnp.bfloat16)),
                ],
                axis=1,
            )
            for k in range(2)
        ]
    )
    attended = attention(normed, query_weight, cosine, sine, kv, blocks)
    mine = lax.dynamic_slice_in_dim(out_weight, side * width, width, 1)
    theirs = lax.dynamic_slice_in_dim(out_weight, (1 - side) * width, width, 1)
    given = jnp.dot(attended, theirs, preferred_element_type=jnp.float32).astype(jnp.bfloat16)
    arrived = swap_heads(given)
    kept = jnp.dot(attended, mine, preferred_element_type=jnp.float32)
    share = kept + arrived.astype(jnp.float32)
    squares = jnp.sum(share * share, axis=1, keepdims=True)
    squares = squares + swap_heads(squares)
    inverse_rms = lax.rsqrt(squares / (2 * width) + norm_epsilon)
    return (tokens.astype(jnp.float32) + post_gain * share * inverse_rms).astype(jnp.bfloat16)


def solution(mesh):
    placed = (
        P("seq", "head"),
        P(),
        P(None, "head"),
        P(None, "head"),
        P(None, "head"),
        P("head", None),
        P("head"),
    )
    return jax.shard_map(
        functools.partial(local, mesh.shape["seq"]),
        mesh=mesh,
        in_specs=placed,
        out_specs=P("seq", "head"),
        check_vma=False,
    )
```

profile of v0, /device:TPU:17, one launch (start us, length us, event | category | flops | bytes accessed | tf_op | source)
XLA Modules:
  0.0 115.0 jit_solution(757382097911143496)
XLA Ops:
  0.0 0.7 collective-permute-start
  0.7 1.3 %broadcast_in_dim.4.gain_ref = f32[1,3584]{1,0:T(1,128)} reshape(f32[3584]{0:T(1024)} %param.8) | data formatting | bytes 28672 | tf_op jit(solution)/shard_map/broadcast_in_dim | solution.py:336
  2.0 2.3 %collective-permute-done.other_ref = bf16[512,1792]{1,0:T(8,128)(2,1)S(1)} collective-permute-done((bf16[512,1792]{1,0:T(8,128)(2,1)}, bf16[512,1792]{1,0:T(8,128)(2,1)S(1)}, u32[]{:S(2)}, u32[]{:S(2)}) %collective-permute-start) | collective-permute-done | bytes 1835040 | tf_op jit(solution)/shard_map/ppermute | solution.py:340
  4.3 1.2 %copy-done.2 = bf16[512,1792]{1,0:T(8,128)(2,1)} copy-done((bf16[512,1792]{1,0:T(8,128)(2,1)}, bf16[512,1792]{1,0:T(8,128)(2,1)S(1)}, u32[]{:S(2)}) %copy-start.2) | copy-done | bytes 1835032
  5.5 5.6 %shard_map.73.normed_ref = bf16[512,3584]{1,0:T(8,128)(2,1)} custom-call(bf16[512,1792]{1,0:T(8,128)(2,1)} %own_ref.1, bf16[512,1792]{1,0:T(8,128)(2,1)} %copy-done.2, f32[1,3584]{1,0:T(1,128)} %broadcast_in_dim.4.gain_ref), custom_call_target="tpu_custom_call" | custom-call | tf_op jit(solution)/shard_map/pallas_call | solution.py:326
  11.1 5.3 %convolution_convert_fusion = bf16[512,512]{1,0:T(8,128)(2,1)S(1)} fusion(bf16[512,3584]{1,0:T(8,128)(2,1)} %shard_map.73.normed_ref, bf16[3584,512]{1,0:T(8,128)(2,1)} %param.11), kind=kOutput, calls=%fused_computation.8 | convolution fusion | flops 1879310336 | bytes 7864320 | tf_op jit(solution)/shard_map/dot_general | solution.py:367
  16.5 0.0 copy-done
  16.5 0.0 copy-done.4
  16.6 2.1 %fusion.28 = f32[512,512]{1,0:T(8,128)S(1)} fusion(bf16[512,3584]{1,0:T(8,128)(2,1)S(1)} %copy-done, bf16[3584,512]{1,0:T(8,128)(2,1)S(1)} %copy-done.4), kind=kOutput, calls=%fused_computation.36 | convolution fusion | flops 1879048192 | bytes 8388608 | tf_op jit(solution)/shard_map/dot_general | solution.py:367
  18.6 1.3 %fusion.18 = (bf16[512,128]{1,0:T(8,128)(2,1)S(1)}, bf16[512,128]{1,0:T(8,128)(2,1)S(1)}, bf16[512,128]{1,0:T(8,128)(2,1)S(1)}, bf16[512,128]{1,0:T(8,128)(2,1)S...) fusion(f32[512,512]{1,0:T(8,128)S(1)} %fusion.28, f32[128]{0:T(128)S(1)} %multiply_exponential_fusion, ...), kind=kLoop, calls=%fused_computation.23 | loop fusion | flops 1114112 | bytes 2099712 | tf_op jit(solution)/shard_map/convert.9
  19.9 0.1 maximum_bitcast_fusion
  20.0 0.0 slice-start
  20.0 0.1 pad_maximum_fusion.kv_ref
  20.1 0.0 slice-start.1
  20.1 77.2 %shard_map.74 = bf16[512,1024]{1,0:T(8,128)(2,1)S(1)} custom-call(bf16[512,3584]{1,0:T(8,128)(2,1)} %shard_map.73.normed_ref, bf16[3584,1024]{1,0:T(8,128)(2,1)} %weight_ref.1, f32[512,128]{1,0:T(8,128)S(1)} %get-tuple-element.12.cosine_ref, f32[512,128]{1,0:T(8,128)S(1)} %get-tuple-element.11.sine_ref, bf16[2,2,2,256,256]{4,3,2,1,0:T(8,128)(2,1)S(1)} %pad_maximum_fusion.kv_ref), custom_call_target="tpu_custom_call" | custom-call | tf_op jit(solution)/shard_map/pallas_call | solution.py:280
  97.4 0.0 slice-done
  97.4 0.0 slice-done.1
  97.4 3.3 %fusion.6 = bf16[512,1792]{1,0:T(8,128)(2,1)} fusion(bf16[512,1024]{1,0:T(8,128)(2,1)S(1)} %shard_map.74, bf16[1024,3584]{1,0:T(8,128)(2,1)S(1)} %bitcast.28, s32[]{:T(128)S(6)} %select_n.7), kind=kOutput, calls=%fused_computation.7 | convolution fusion | flops 1879965696 | bytes 6553604 | tf_op jit(solution)/shard_map/dot_general | solution.py:386
  100.7 3.2 %collective-permute-start.1 = (bf16[512,1792]{1,0:T(8,128)(2,1)}, bf16[512,1792]{1,0:T(8,128)(2,1)S(1)}, u32[]{:S(2)}, u32[]{:S(2)}) collective-permute-start(bf16[512,1792]{1,0:T(8,128)(2,1)} %fusion.6), channel_id=1, source_target_pairs={{0,1},{1,0},{2,3},{3,2},{4,5},{5,4},{6,7},{7,6},{8,9},{9,8},{10,11... | collective-permute-start | bytes 5505032 | tf_op jit(solution)/shard_map/ppermute | solution.py:340
  103.9 3.6 %collective-permute-done.1 = bf16[512,1792]{1,0:T(8,128)(2,1)S(1)} collective-permute-done((bf16[512,1792]{1,0:T(8,128)(2,1)}, bf16[512,1792]{1,0:T(8,128)(2,1)S(1)}, u32[]{:S(2)}, u32[]{:S(2)}) %collective-permute-start.1) | collective-permute-done | bytes 1835040 | tf_op jit(solution)/shard_map/ppermute | solution.py:340
  107.6 4.2 %multiply_reduce_fusion = (f32[512]{0:T(512)S(1)}, f32[512,1792]{1,0:T(8,128)S(1)}) fusion(bf16[512,1792]{1,0:T(8,128)(2,1)S(1)} %collective-permute-done.1, bf16[512,1024]{1,0:T(8,128)(2,1)S(1)} %shard_map.74, bf16[1024,3584]{1,0:T(8,128)(2,1)} %param.12, s32[]{:T(128)S(6)} %select_n.6), kind=kOutput, calls=%fused_computation.1 | convolution fusion | flops 1882717696 | bytes 10225668 | tf_op jit(solution)/shard_map/dot_general | solution.py:388
  111.8 0.4 collective-permute-start.2
  112.2 0.8 collective-permute-done.2
  113.1 1.9 %add_convert_fusion = bf16[512,1792]{1,0:T(8,128)(2,1)} fusion(f32[512,1792]{1,0:T(8,128)S(1)} %get-tuple-element.14, bf16[512,1792]{1,0:T(8,128)(2,1)S(1)} %copy-done.1, f32[512]{0:T(512)S(1)} %bitcast.24, f32[1792]{0:T(1024)S(1)} %copy-done.3), kind=kLoop, calls=%fused_computation | loop fusion | flops 4587520 | bytes 7349248 | tf_op jit(solution)/shard_map/convert_element_type | solution.py:393
  (12 shorter events, 0.1 us)
Async XLA Ops:
  0.0 4.3 %collective-permute-start = (bf16[512,1792]{1,0:T(8,128)(2,1)}, bf16[512,1792]{1,0:T(8,128)(2,1)S(1)}, u32[]{:S(2)}, u32[]{:S(2)}) collective-permute-start(bf16[512,1792]{1,0:T(8,128)(2,1)} %own_ref.1), channel_id=1, source_target_pairs={{0,1},{1,0},{2,3},{3,2},{4,5},{5,4},{6,7},{7,6},{8,9},{9,8},{10,11... | collective-permute-start | bytes 5505032 | tf_op jit(solution)/shard_map/ppermute | solution.py:340
  4.3 1.2 %copy-start.2 = (bf16[512,1792]{1,0:T(8,128)(2,1)}, bf16[512,1792]{1,0:T(8,128)(2,1)S(1)}, u32[]{:S(2)}) copy-start(bf16[512,1792]{1,0:T(8,128)(2,1)S(1)} %collective-permute-done.other_ref) | copy-start | bytes 5505028
  11.1 5.4 %copy-start = (bf16[512,3584]{1,0:T(8,128)(2,1)S(1)}, bf16[512,3584]{1,0:T(8,128)(2,1)}, u32[]{:S(2)}) copy-start(bf16[512,3584]{1,0:T(8,128)(2,1)} %shard_map.73.normed_ref) | copy-start | bytes 11010052
  11.1 5.4 %copy-start.4 = (bf16[3584,512]{1,0:T(8,128)(2,1)S(1)}, bf16[3584,512]{1,0:T(8,128)(2,1)}, u32[]{:S(2)}) copy-start(bf16[3584,512]{1,0:T(8,128)(2,1)} %param.10) | copy-start | bytes 11010052
  20.0 77.4 %slice-start = ((s8[7340032]{0:T(1024)(128)(4,1)}), s8[4194304]{0:T(1024)(128)(4,1)S(1)}, s32[]{:S(2)}) async-start(s8[7340032]{0:T(1024)(128)(4,1)} %bitcast.27), calls=%async_computation | async-start | bytes 8388608
  20.1 77.3 %slice-start.1 = ((s8[7340032]{0:T(1024)(128)(4,1)}), s8[3145728]{0:T(1024)(128)(4,1)S(1)}, s32[]{:S(2)}) async-start(s8[7340032]{0:T(1024)(128)(4,1)} %bitcast.27), calls=%async_computation.1 | async-start | bytes 6291456
  100.7 6.9 %collective-permute-start.1 = (bf16[512,1792]{1,0:T(8,128)(2,1)}, bf16[512,1792]{1,0:T(8,128)(2,1)S(1)}, u32[]{:S(2)}, u32[]{:S(2)}) collective-permute-start(bf16[512,1792]{1,0:T(8,128)(2,1)} %fusion.6), channel_id=1, source_target_pairs={{0,1},{1,0},{2,3},{3,2},{4,5},{5,4},{6,7},{7,6},{8,9},{9,8},{10,11... | collective-permute-start | bytes 5505032 | tf_op jit(solution)/shard_map/ppermute | solution.py:340
  103.9 9.1 %copy-start.1 = (bf16[512,1792]{1,0:T(8,128)(2,1)S(1)}, bf16[512,1792]{1,0:T(8,128)(2,1)}, u32[]{:S(2)}) copy-start(bf16[512,1792]{1,0:T(8,128)(2,1)} %own_ref.1) | copy-start | bytes 5505028
  103.9 9.1 %copy-start.3 = (f32[1792]{0:T(1024)S(1)}, f32[1792]{0:T(1024)}, u32[]{:S(2)}) copy-start(f32[1792]{0:T(1024)} %param.13) | copy-start | bytes 21508
  111.8 1.3 %collective-permute-start.2 = (f32[512,1]{0,1:T(1,128)S(1)}, f32[512,1]{0,1:T(1,128)S(1)}, u32[]{:S(2)}, u32[]{:S(2)}) collective-permute-start(f32[512,1]{0,1:T(1,128)S(1)} %bitcast.25), channel_id=1, source_target_pairs={{0,1},{1,0},{2,3},{3,2},{4,5},{5,4},{6,7},{7,6},{8,9},{9,8},{10,11... | collective-permute-start | bytes 6152 | tf_op jit(solution)/shard_map/ppermute | solution.py:340
where the time goes:
time: 115 us
  Pallas kernels  82.9 us (72%)
  matrix products  14.9 us (13%)
  waiting for transfers between devices  6.72 us (6%)
  starting transfers between devices  4.35 us (4%)
  other arithmetic  3.39 us (3%)
  local copies, waits for them, and re-layouts  2.61 us (2%)
    pallas_call x1, Pallas kernels, attention(): pl.pallas_call(functools.partial(attention_kernel, blocks, rows), out_sha...  77.2 us
    dot_general x2, matrix products, local(): jnp.dot(normed, weight, preferred_element_type=jnp.float32)  7.39 us
    ppermute x3, waiting for transfers between devices, swap_heads(): return lax.ppermute(shard, 'head', [(0, 1), (1, 0)])  6.72 us
    pallas_call x1, Pallas kernels, norm(): pl.pallas_call(norm_kernel, grid=(rows // step,), out_shape=jax.ShapeDtyp...  5.61 us
    ppermute x3, starting transfers between devices, swap_heads(): return lax.ppermute(shard, 'head', [(0, 1), (1, 0)])  4.35 us
    dot_general x1, matrix products, local(): kept = jnp.dot(attended, mine, preferred_element_type=jnp.float32)  4.2 us
    dot_general x1, matrix products, local(): jnp.dot(attended, theirs, preferred_element_type=jnp.float32)  3.3 us
  transfers between devices with their start and end apart: 3, of which 3 were waited for; matrix products, arithmetic and copies ran while one was open for 1% of the time, Pallas kernels for 0%

commit v1 on v0

v1 whole, which is shorter than its diff:
```python
import functools
import math

import jax
import jax.numpy as jnp
import numpy as np
from jax import lax
from jax.experimental import pallas as pl
from jax.experimental.pallas import tpu as pltpu
from jax.sharding import PartitionSpec as P

HD = 256
LANES = 128
WINDOW = 4096

softcap_limit = 50.0
rope_base = 10000.0
norm_epsilon = 1e-06

CHUNKS = 4
UNITS = 2

TOKEN = 0
X_KV = TOKEN + CHUNKS
X_Q = X_KV + CHUNKS
X_OUT = X_Q + 1
Z_NEAR = X_OUT + CHUNKS
Z_FAR = Z_NEAR + 2 * CHUNKS
Y_NEAR = Z_FAR + 2 * CHUNKS
Y_FAR = Y_NEAR + 2 * CHUNKS
GIVEN = Y_FAR + 2 * CHUNKS
SQUARES = GIVEN + CHUNKS
MESSAGES = SQUARES + CHUNKS

L_TOKEN = 0
L_GAIN = L_TOKEN + CHUNKS
L_FREQ = L_GAIN + 1
L_POST = L_FREQ + 1
L_KV = L_POST + 1
L_Q = L_KV + 8
L_OUT = L_Q + 4
LOCALS = L_OUT + 4

inner = 1.0 / (math.sqrt(HD) * softcap_limit)
outer = softcap_limit / math.log(2.0)


def rotated(head, cosine, sine):
    midpoint = HD // 2
    leading, trailing = head[:, :midpoint], head[:, midpoint:]
    return jnp.concatenate(
        [leading * cosine - trailing * sine, trailing * cosine + leading * sine], axis=-1
    ).astype(jnp.bfloat16)


def layer_kernel(
    blocks, tokens_hbm, gain_hbm, freq_hbm, wq_hbm, wk_hbm, wv_hbm, wo_hbm, post_hbm, out_ref,
    own, other, gain, freq, post, normed, wkv, wq, wo, cosine, sine, held, kvm, queries, asked,
    total, mass, leaving, landed, finished, branch, given, arrived, sq_own, sq_other,
    send_sems, recv_sems, local_sems,
):
    rows, width = own.shape
    part = rows // CHUNKS
    unit = rows // UNITS
    group = 2 * 2
    me = lax.axis_index("seq")
    side = lax.axis_index("head")
    x = me % 2
    y = (me // 2) % 2
    x_mate = me + 1 - 2 * x
    y_mate = me + 2 - 4 * y
    z_next = me + group
    has_next = z_next < blocks
    has_prev = me >= group
    has_far = me >= 2 * group
    first_row = y == 0
    second_row = y == 1

    def local(index, src, dst):
        return pltpu.make_async_copy(src, dst, local_sems.at[index])

    def copy(message, src, dst, device):
        return pltpu.make_async_remote_copy(
            src_ref=src,
            dst_ref=dst,
            send_sem=send_sems.at[message],
            recv_sem=recv_sems.at[message],
            device_id=device,
            device_id_type=pl.DeviceIdType.MESH,
        )

    to_x = {"seq": x_mate}
    to_y = {"seq": y_mate}
    to_z = {"seq": z_next}
    to_core = {"head": 1 - side}

    def chunk(p):
        return pl.ds(pl.multiple_of(p * part, part), part)

    halves = (side, 1 - side)
    pairs = (x, 1 - x)

    own_copy = [local(L_TOKEN + p, tokens_hbm.at[chunk(p)], own.at[chunk(p)]) for p in range(CHUNKS)]
    gain_copy = local(L_GAIN, gain_hbm, gain)
    freq_copy = local(L_FREQ, freq_hbm, freq)
    post_copy = local(L_POST, post_hbm, post)
    kv_copies = [[], []]
    q_copies = [[], []]
    out_copies = [[], []]
    for i in range(2):
        for f in range(2):
            at_rows = pl.ds(pl.multiple_of(halves[f] * width, width), width)
            for n, source in enumerate((wk_hbm, wv_hbm)):
                columns = pl.ds(pl.multiple_of(pairs[i] * HD, HD), HD)
                kv_copies[i].append(
                    local(
                        L_KV + 4 * i + 2 * f + n,
                        source.at[at_rows, columns],
                        wkv.at[i, pl.ds(f * width, width), pl.ds(n * HD, HD)],
                    )
                )
            columns = pl.ds(pl.multiple_of(pairs[i] * 2 * HD, 2 * HD), 2 * HD)
            q_copies[i].append(
                local(
                    L_Q + 2 * i + f,
                    wq_hbm.at[at_rows, columns],
                    wq.at[i, pl.ds(f * width, width), :],
                )
            )
            at_heads = pl.ds(pl.multiple_of(pairs[i] * 2 * HD, 2 * HD), 2 * HD)
            columns = pl.ds(pl.multiple_of(halves[1 - f] * width, width), width)
            out_copies[i].append(local(L_OUT + 2 * i + f, wo_hbm.at[at_heads, columns], wo.at[i, f]))

    order = [CHUNKS - 1 - i for i in range(CHUNKS)]
    for p in order:
        own_copy[p].start()
    freq_copy.start()
    gain_copy.start()
    for c in kv_copies[0]:
        c.start()

    barrier = pltpu.get_barrier_semaphore()

    def greet(device):
        pl.semaphore_signal(barrier, inc=1, device_id=device, device_id_type=pl.DeviceIdType.MESH)

    greet(to_core)
    greet(to_x)
    greet(to_y)
    pl.when(has_next)(lambda: greet(to_z))
    pl.when(has_prev)(lambda: greet({"seq": me - group}))
    pl.semaphore_wait(barrier, 3 + has_next.astype(jnp.int32) + has_prev.astype(jnp.int32))

    def token_copy(p):
        return copy(TOKEN + p, tokens_hbm.at[chunk(p)], other.at[chunk(p)], to_core)

    for p in order:
        token_copy(p).start()
    for c in kv_copies[1]:
        c.start()
    for i in (1, 0):
        for c in q_copies[i]:
            c.start()

    def piece(ref, p):
        return ref.at[:, chunk(p), :]

    def of(r):
        return x + r - 2 * x * r

    def send_x(p):
        return copy(X_KV + p, piece(kvm, p), piece(held.at[0, x], p), to_x)

    def take_x(p):
        return copy(X_KV + p, piece(kvm, p), piece(held.at[0, 1 - x], p), to_x)

    def place(r, p):
        return r * CHUNKS + CHUNKS - 1 - p

    def z_near(r, p):
        b = of(r)
        return copy(Z_NEAR + place(r, p), piece(held.at[0, b], p), piece(held.at[2, b], p), to_z)

    def z_far(b, p):
        return copy(Z_FAR + place(1 - b, p), piece(held.at[2, b], p), piece(held.at[4, b], p), to_z)

    def y_near(slot, r, p):
        b = of(r)
        return copy(Y_NEAR + place(r, p), piece(held.at[slot, b], p), piece(held.at[1, b], p), to_y)

    def y_far(slot, b, p):
        return copy(Y_FAR + place(1 - b, p), piece(held.at[slot, b], p), piece(held.at[3, b], p), to_y)

    freq_copy.wait()
    at_row = lax.broadcasted_iota(jnp.int32, (rows, LANES), 0) + me * rows
    angles = at_row.astype(jnp.float32) * freq[...]
    cosine[...] = jnp.cos(angles)
    sine[...] = jnp.sin(angles)
    total[...] = jnp.zeros_like(total)
    mass[...] = jnp.zeros_like(mass)
    gain_copy.wait()

    lines = 16
    tiles = width // LANES

    def norm_chunk(p):
        def step(i, carry):
            at = pl.ds(pl.multiple_of(p * part + i * lines, lines), lines)
            squares = None
            for ref in (own, other):
                for j in range(tiles):
                    value = ref[at, j * LANES : (j + 1) * LANES].astype(jnp.float32)
                    squares = value * value if squares is None else squares + value * value
            scale = lax.rsqrt(
                jnp.sum(squares, axis=-1, keepdims=True) / (2 * width) + norm_epsilon
            )
            scale = jnp.broadcast_to(scale, (lines, LANES))
            for f, ref in enumerate((own, other)):
                for j in range(tiles):
                    value = ref[at, j * LANES : (j + 1) * LANES].astype(jnp.float32)
                    weight = gain[pl.ds(halves[f] * tiles + j, 1), :]
                    to = f * width + j * LANES
                    normed[at, to : to + LANES] = (value * scale * weight).astype(jnp.bfloat16)
            return carry

        lax.fori_loop(0, part // lines, step, 0)

    def project_kv(p, i, dst):
        value = jnp.dot(normed[chunk(p), :], wkv[i], preferred_element_type=jnp.float32)
        key = rotated(value[:, :HD], cosine[chunk(p), :], sine[chunk(p), :])
        dst[0, chunk(p), :] = key
        dst[1, chunk(p), :] = value[:, HD:].astype(jnp.bfloat16)

    def take_near(r, p):
        def act():
            z_near(r, p).wait_recv()
            pl.when(second_row)(lambda: y_near(2, r, p).start())

        pl.when(has_prev)(act)

    def pass_far(b, p):
        def act():
            pl.when(has_next)(lambda: z_far(b, p).start())
            pl.when(first_row)(lambda: y_far(2, b, p).start())

        pl.when(has_prev)(act)

    def take_far(b, p):
        def act():
            z_far(b, p).wait_recv()
            pl.when(second_row)(lambda: y_far(4, b, p).start())

        pl.when(has_far)(act)

    def pass_mate(p):
        take_x(p).wait_recv()
        pl.when(has_next)(lambda: z_near(1, p).start())
        pl.when(first_row)(lambda: y_near(0, 1, p).start())

    for i, p in enumerate(order):
        own_copy[p].wait()
        token_copy(p).wait_recv()
        norm_chunk(p)
        if i == 0:
            for c in kv_copies[0]:
                c.wait()
        project_kv(p, 0, held.at[0, x])
        pl.when(has_next)(lambda: z_near(0, p).start())
        pl.when(first_row)(lambda: y_near(0, 0, p).start())
        if i == 0:
            for c in kv_copies[1]:
                c.wait()
        project_kv(p, 1, kvm)
        send_x(p).start()
        if i == 0:
            for i_ in (0, 1):
                for c in out_copies[i_]:
                    c.start()
            post_copy.start()
        if i == 2:
            take_near(0, order[0])

    def project_q(i, dst):
        def step(t, carry):
            at = pl.ds(pl.multiple_of(t * unit, unit), unit)
            value = jnp.dot(normed[at, :], wq[i], preferred_element_type=jnp.float32)
            for head in range(2):
                dst[pl.ds(pl.multiple_of(head * rows + t * unit, unit), unit), :] = rotated(
                    value[:, head * HD : (head + 1) * HD], cosine[at, :], sine[at, :]
                )
            return carry

        lax.fori_loop(0, UNITS, step, 0)

    def q_copy():
        return copy(X_Q, asked, queries.at[1], to_x)

    pass_mate(order[0])
    for c in q_copies[1]:
        c.wait()
    take_near(0, order[1])
    project_q(1, asked)
    q_copy().start()
    pass_mate(order[1])
    take_near(0, order[2])
    for c in q_copies[0]:
        c.wait()
    project_q(0, queries.at[0])
    pass_mate(order[2])
    take_near(0, order[3])
    pass_mate(order[3])

    def attend(which, slot, b, h, distance=None):
        at = pl.ds(pl.multiple_of(h * unit, unit), unit)
        scores = lax.dot_general(
            queries[which],
            held[slot, b, 0, at, :],
            (((1,), (1,)), ((), ())),
            preferred_element_type=jnp.float32,
        )
        weights = jnp.exp2(outer * jnp.tanh(scores * inner))
        if distance is not None:
            down = lax.broadcasted_iota(jnp.int32, weights.shape, 0)
            down = jnp.where(down >= rows, down - rows, down)
            offset = (distance - h * unit) + down - lax.broadcasted_iota(jnp.int32, weights.shape, 1)
            weights = jnp.where((offset >= 0) & (offset < WINDOW), weights, 0.0)
        added = None
        for k in range(unit // LANES):
            lanes = weights[:, k * LANES : (k + 1) * LANES]
            added = lanes if added is None else added + lanes
        mass[which] += added
        total[which] += jnp.dot(
            weights.astype(jnp.bfloat16), held[slot, b, 1, at, :], preferred_element_type=jnp.float32
        )

    def both(act):
        def step(s, carry):
            act(s)
            return carry

        lax.fori_loop(0, 2, step, 0)

    def attend_own(which):
        mine = of(which)

        def step(i, carry):
            b = mine - i // UNITS
            attend(which, 0, b, i % UNITS, (mine - b) * rows)
            return carry

        lax.fori_loop(0, UNITS + UNITS * mine, step, 0)

    def z_unit(u):
        return 2, of(u // UNITS), UNITS - 1 - u % UNITS

    def y_unit(w):
        far = w // 4
        r = (w % 4) // UNITS
        b = (1 - far) * of(r) + far * (1 - r)
        return 1 + 2 * far, b, UNITS - 1 - w % UNITS

    def y_there(w):
        return me >= 2 + 4 * (w // 4)

    def take_y(w):
        slot, b, h = y_unit(w)
        for n in range(CHUNKS // UNITS):
            k = CHUNKS // UNITS * w + n
            p = CHUNKS - 1 - k % CHUNKS
            copy(Y_NEAR + k, piece(held.at[slot, b], p), piece(held.at[slot, b], p), to_y).wait_recv()

    attend_own(0)

    def near_step(u, carry):
        p = CHUNKS - 1 - u
        take_near(1, p)
        pass_far(1, p)
        pl.when(has_prev)(lambda: attend(0, *z_unit(u)))

        def with_y():
            take_y(u - 1)
            attend(0, *y_unit(u - 1))

        pl.when((u >= 1) & y_there(0))(with_y)
        return carry

    lax.fori_loop(0, 4, near_step, 0)
    for p in order:
        pass_far(0, p)

    q_copy().wait_recv()
    attend_own(1)
    take_far(1, order[0])

    def again_z(u, carry):
        attend(1, *z_unit(u))
        return carry

    def repeat(count, step):
        def act():
            lax.fori_loop(0, count, step, 0)

        return act

    pl.when(has_prev)(repeat(4, again_z))
    take_far(1, order[1])

    def again_y(w, carry):
        attend(1, *y_unit(w))
        return carry

    pl.when(y_there(0))(repeat(3, again_y))

    def whole_y(w):
        def act():
            take_y(w)
            both(lambda s: attend(s, *y_unit(w)))

        pl.when(y_there(w))(act)

    def take_next(k):
        def act():
            take_far(1 - k // CHUNKS, CHUNKS - 1 - k % CHUNKS)

        pl.when(k < 2 * CHUNKS)(act)

    def far_step(v, carry):
        whole_y(3 + v)
        take_next(2 + 2 * v)

        def far_unit():
            b = 1 - v // UNITS

            def one(s):
                mine = of(s)
                pl.when(mine <= b)(
                    lambda: attend(s, 4, b, UNITS - 1 - v % UNITS, WINDOW + (mine - b) * rows)
                )

            both(one)

        pl.when(has_far)(far_unit)
        take_next(3 + 2 * v)
        return carry

    lax.fori_loop(0, 4, far_step, 0)
    whole_y(7)

    def finish(which, head, at_rows):
        at = pl.ds(head * rows + at_rows.start, at_rows.size)
        weight = jnp.sum(mass[which, at, :], axis=-1, keepdims=True)
        return (total[which, at, :] * (1.0 / weight)).astype(jnp.bfloat16)

    def out_copy(p):
        return copy(X_OUT + p, leaving.at[chunk(p)], landed.at[chunk(p)], to_x)

    for p in range(CHUNKS):
        for head in range(2):
            leaving[chunk(p), head * HD : (head + 1) * HD] = finish(1, head, chunk(p))
        out_copy(p).start()
    for p in range(CHUNKS):
        for head in range(2):
            finished[chunk(p), head * HD : (head + 1) * HD] = finish(0, head, chunk(p))
    for i in (0, 1):
        for c in out_copies[i]:
            c.wait()
    post_copy.wait()

    for f in range(2):
        def column(t, carry):
            at = pl.ds(pl.multiple_of(t * HD, HD), HD)
            branch[f, :, at] = jnp.dot(
                finished[...], wo[0, f, :, at], preferred_element_type=jnp.float32
            )
            return carry

        lax.fori_loop(0, width // HD, column, 0)

    def given_copy(p):
        return copy(GIVEN + p, given.at[chunk(p)], arrived.at[chunk(p)], to_core)

    def squares_copy(p):
        return copy(SQUARES + p, sq_own.at[chunk(p)], sq_other.at[chunk(p)], to_core)

    def add_mate(p):
        out_copy(p).wait_recv()
        theirs = landed[chunk(p), :]
        given[chunk(p), :] = (
            branch[0, chunk(p), :]
            + jnp.dot(theirs, wo[1, 0], preferred_element_type=jnp.float32)
        ).astype(jnp.bfloat16)
        given_copy(p).start()
        branch[1, chunk(p), :] += jnp.dot(theirs, wo[1, 1], preferred_element_type=jnp.float32)

    def add_core(p):
        given_copy(p).wait_recv()
        squares = None
        for j in range(tiles):
            at = slice(j * LANES, (j + 1) * LANES)
            share = branch[1, chunk(p), at] + arrived[chunk(p), at].astype(jnp.float32)
            branch[1, chunk(p), at] = share
            squares = share * share if squares is None else squares + share * share
        sq_own[chunk(p), :] = squares
        squares_copy(p).start()

    def last(p):
        squares_copy(p).wait_recv()
        squares = jnp.sum(sq_own[chunk(p), :] + sq_other[chunk(p), :], axis=-1, keepdims=True)
        scale = jnp.broadcast_to(
            lax.rsqrt(squares / (2 * width) + norm_epsilon), (part, LANES)
        )
        for j in range(tiles):
            at = slice(j * LANES, (j + 1) * LANES)
            out_ref[chunk(p), at] = (
                own[chunk(p), at].astype(jnp.float32)
                + post[j : j + 1, :] * branch[1, chunk(p), at] * scale
            ).astype(jnp.bfloat16)

    def tail(p, carry):
        pl.when(p < CHUNKS)(lambda: add_mate(p))
        pl.when((p >= 1) & (p < CHUNKS + 1))(lambda: add_core(p - 1))
        pl.when(p >= 2)(lambda: last(p - 2))
        return carry

    lax.fori_loop(0, CHUNKS + 2, tail, 0)

    q_copy().wait_send()
    for p in order:
        token_copy(p).wait_send()
        send_x(p).wait_send()
        out_copy(p).wait_send()
        given_copy(p).wait_send()
        squares_copy(p).wait_send()
    for r in range(2):
        for p in order:
            pl.when(has_next)(lambda: z_near(r, p).wait_send())
            pl.when(has_next & has_prev)(lambda: z_far(r, p).wait_send())
            pl.when(first_row)(lambda: y_near(0, r, p).wait_send())
            pl.when(first_row & has_prev)(lambda: y_far(2, r, p).wait_send())
            pl.when(second_row & has_prev)(lambda: y_near(2, r, p).wait_send())
            pl.when(second_row & has_far)(lambda: y_far(4, r, p).wait_send())


def local_layer(blocks, tokens, pre_gain, query_weight, key_weight, value_weight, out_weight, post_gain):
    rows, width = tokens.shape
    frequency = np.exp(-np.log(rope_base) * (2.0 * np.arange(HD // 2) / HD)).astype(np.float32)
    anywhere = pl.BlockSpec(memory_space=pl.ANY)
    bf16, f32 = jnp.bfloat16, jnp.float32
    vmem = pltpu.VMEM
    half = 2 * HD
    return pl.pallas_call(
        functools.partial(layer_kernel, blocks),
        out_shape=jax.ShapeDtypeStruct((rows, width), bf16),
        in_specs=[anywhere] * 8,
        out_specs=pl.BlockSpec(memory_space=pltpu.VMEM),
        scratch_shapes=[
            vmem((rows, width), bf16),
            vmem((rows, width), bf16),
            vmem((2 * width // LANES, LANES), f32),
            vmem((1, LANES), f32),
            vmem((width // LANES, LANES), f32),
            vmem((rows, 2 * width), bf16),
            vmem((2, 2 * width, half), bf16),
            vmem((2, 2 * width, half), bf16),
            vmem((2, 2, half, width), bf16),
            vmem((rows, LANES), f32),
            vmem((rows, LANES), f32),
            vmem((5, 2, 2, rows, HD), bf16),
            vmem((2, rows, HD), bf16),
            vmem((2, 2 * rows, HD), bf16),
            vmem((2 * rows, HD), bf16),
            vmem((2, 2 * rows, HD), f32),
            vmem((2, 2 * rows, LANES), f32),
            vmem((rows, half), bf16),
            vmem((rows, half), bf16),
            vmem((rows, half), bf16),
            vmem((2, rows, width), f32),
            vmem((rows, width), bf16),
            vmem((rows, width), bf16),
            vmem((rows, LANES), f32),
            vmem((rows, LANES), f32),
            pltpu.SemaphoreType.DMA((MESSAGES,)),
            pltpu.SemaphoreType.DMA((MESSAGES,)),
            pltpu.SemaphoreType.DMA((LOCALS,)),
        ],
        compiler_params=pltpu.CompilerParams(
            collective_id=0, has_side_effects=True, vmem_limit_bytes=62 * 1024 * 1024
        ),
    )(
        tokens,
        pre_gain.reshape(-1, LANES),
        jnp.asarray(frequency)[None, :],
        query_weight,
        key_weight,
        value_weight,
        out_weight,
        post_gain.reshape(-1, LANES),
    )


def solution(mesh):
    placed = (
        P("seq", "head"),
        P(),
        P(None, "head"),
        P(None, "head"),
        P(None, "head"),
        P("head", None),
        P("head"),
    )
    return jax.shard_map(
        functools.partial(local_layer, mesh.shape["seq"]),
        mesh=mesh,
        in_specs=placed,
        out_specs=P("seq", "head"),
        check_vma=False,
    )
```

time: 115 us -> 82.2 us (0.71)
  matrix products: 14.9 us -> 0 us
  waiting for transfers between devices: 6.72 us -> 0 us
  starting transfers between devices: 4.35 us -> 0 us
  Pallas kernels: 82.9 us -> 79.2 us
  other arithmetic: 3.39 us -> 0 us
    dot_general x4 -> x0, matrix products: 14.9 us -> none  [the longest x2 7.39 us: local(): jnp.dot(normed, weight, preferred_element_type=jnp.float32)]
    ppermute x3 -> x0, waiting for transfers between devices: 6.72 us -> none  [swap_heads(): return lax.ppermute(shard, 'head', [(0, 1), (1, 0)])]
    ppermute x3 -> x0, starting transfers between devices: 4.35 us -> none  [swap_heads(): return lax.ppermute(shard, 'head', [(0, 1), (1, 0)])]
    pallas_call x2 -> x1, Pallas kernels: 82.9 us -> 79.2 us  [local_layer(): pl.pallas_call(functools.partial(layer_kernel, blocks), out_shape=jax.Sha...]
    convert_element_type x2 -> x0, other arithmetic: 1.91 us -> none  [the longest x1 1.9 us: local(): (tokens.astype(jnp.float32) + post_gain * share * inverse_rms).astype(jnp...]
    unnamed x14 -> x1, local copies, waits for them, and re-layouts: 1.26 us -> 2.85 us
    another operation x3 -> x0, other arithmetic: 1.47 us -> none
    broadcast_in_dim x1 -> x0, local copies, waits for them, and re-layouts: 1.32 us -> none  [norm(): gain[None, :]]
  transfers between devices with their start and end apart: 3 -> 0, of which waited for: 3 -> 0; matrix products, arithmetic and copies ran while one was open for 1% -> 0% of each run, Pallas kernels for 0% -> 0%
where the time goes in v1:
time: 82.2 us; the launch traced here: 82 us
  Pallas kernels  79.2 us (96%)
  local copies, waits for them, and re-layouts  2.85 us (3%)
    pallas_call x1, Pallas kernels, local_layer(): pl.pallas_call(functools.partial(layer_kernel, blocks), out_shape=jax.Sha...  79.2 us
    unnamed x1, local copies, waits for them, and re-layouts  2.85 us

profile of v1, /device:TPU:17, one launch (start us, length us, event | category | flops | bytes accessed | tf_op | source)
XLA Modules:
  0.0 82.0 jit_solution(14187678322896783394)
XLA Ops:
  0.0 79.2 %shard_map.82 = bf16[512,1792]{1,0:T(8,128)(2,1)} custom-call(bf16[512,1792]{1,0:T(8,128)(2,1)} %tokens_hbm.1, f32[28,128]{1,0:T(8,128)} %bitcast.2, f32[1,128]{1,0:T(1,128)} %constant.3.freq_hbm, bf16[3584,1024]{1,0:T(8,128)(2,1)} %wq_hbm.1, bf16[3584,512]{1,0:T(8,128)(2,1)} %wk_hbm.1, bf16[3584,512]{1,0:T(8,128)(2,1)} %wv_hbm.1, ...), custom_call_target="tpu_custom_call" | custom-call | tf_op jit(solution)/shard_map/pallas_call | solution.py:551
  79.2 2.8 %copy.10 = bf16[512,1792]{1,0:T(8,128)(2,1)} copy(bf16[512,1792]{1,0:T(8,128)(2,1)} %shard_map.82) | data formatting | bytes 3670016

commit v2 on v1

v2 whole, which is shorter than its diff:
```python
import functools
import math

import jax
import jax.numpy as jnp
import numpy as np
from jax import lax
from jax.experimental import pallas as pl
from jax.experimental.pallas import tpu as pltpu
from jax.sharding import PartitionSpec as P

HD = 256
LANES = 128
WINDOW = 4096

softcap_limit = 50.0
rope_base = 10000.0
norm_epsilon = 1e-06

CHUNKS = 4
UNITS = 2

TOKEN = 0
X_KV = TOKEN + CHUNKS
X_Q = X_KV + CHUNKS
X_OUT = X_Q + 1
Z_NEAR = X_OUT + CHUNKS
Z_FAR = Z_NEAR + 2 * CHUNKS
Z_EXTRA = Z_FAR + CHUNKS + CHUNKS // 2
Y_NEAR = Z_EXTRA + CHUNKS // 2
Y_FAR = Y_NEAR + 2 * UNITS
Y_EXTRA = Y_FAR + 2 * UNITS
GIVEN = Y_EXTRA + 1
SQUARES = GIVEN + CHUNKS
MESSAGES = SQUARES + CHUNKS

(
    S_TOKEN, S_X, S_Q, S_OUT, S_Z_NEAR, S_Z_FAR, S_Y_NEAR, S_Y_FAR, S_Y_LATE, S_Y_EXTRA, S_GIVEN,
    S_SQUARES, SENDS,
) = range(13)

L_TOKEN = 0
L_GAIN = L_TOKEN + CHUNKS
L_FREQ = L_GAIN + 1
L_POST = L_FREQ + 1
L_KV = L_POST + 1
L_Q = L_KV + 2
L_OUT = L_Q + 2
LOCALS = L_OUT + 1

inner = 1.0 / (math.sqrt(HD) * softcap_limit)
outer = softcap_limit / math.log(2.0)


def rotated(head, cosine, sine):
    midpoint = HD // 2
    leading, trailing = head[:, :midpoint], head[:, midpoint:]
    return jnp.concatenate(
        [leading * cosine - trailing * sine, trailing * cosine + leading * sine], axis=-1
    ).astype(jnp.bfloat16)


def layer_kernel(
    blocks, tokens_hbm, gain_hbm, freq_hbm, wq_hbm, wk_hbm, wv_hbm, wo_hbm, post_hbm, out_ref,
    own, other, gain, freq, post, normed, wkv, wq, wo, cosine, sine, held, kvm, queries, asked,
    total, mass, leaving, landed, finished, branch, arrived, sq_own, sq_other,
    send_sems, recv_sems, local_sems,
):
    rows, width = own.shape
    part = rows // CHUNKS
    unit = rows // UNITS
    group = 2 * 2
    me = lax.axis_index("seq")
    side = lax.axis_index("head")
    x = me % 2
    y = (me // 2) % 2
    x_mate = me + 1 - 2 * x
    y_mate = me + 2 - 4 * y
    z_next = me + group
    has_next = z_next < blocks
    has_prev = me >= group
    has_far = me >= 2 * group
    first_row = y == 0
    second_row = y == 1

    def local(index, src, dst):
        return pltpu.make_async_copy(src, dst, local_sems.at[index])

    def copy(kind, message, src, dst, device):
        return pltpu.make_async_remote_copy(
            src_ref=src,
            dst_ref=dst,
            send_sem=send_sems.at[kind],
            recv_sem=recv_sems.at[message],
            device_id=device,
            device_id_type=pl.DeviceIdType.MESH,
        )

    to_x = {"seq": x_mate}
    to_y = {"seq": y_mate}
    to_z = {"seq": z_next}
    to_core = {"head": 1 - side}

    def chunk(p):
        return pl.ds(pl.multiple_of(p * part, part), part)

    given = other
    sums = (branch, out_ref)
    halves = (side, 1 - side)
    pairs = (x, 1 - x)

    own_copy = [local(L_TOKEN + p, tokens_hbm.at[chunk(p)], own.at[chunk(p)]) for p in range(CHUNKS)]
    gain_copy = local(L_GAIN, gain_hbm, gain)
    freq_copy = local(L_FREQ, freq_hbm, freq)
    post_copy = local(L_POST, post_hbm, post)
    kv_copies = [[], []]
    q_copies = [[], []]
    out_copies = [[], []]
    for i in range(2):
        for f in range(2):
            at_rows = pl.ds(pl.multiple_of(halves[f] * width, width), width)
            for n, source in enumerate((wk_hbm, wv_hbm)):
                columns = pl.ds(pl.multiple_of(pairs[i] * HD, HD), HD)
                kv_copies[i].append(
                    local(
                        L_KV + i,
                        source.at[at_rows, columns],
                        wkv.at[i, pl.ds(f * width, width), pl.ds(n * HD, HD)],
                    )
                )
            columns = pl.ds(pl.multiple_of(pairs[i] * 2 * HD, 2 * HD), 2 * HD)
            q_copies[i].append(
                local(
                    L_Q + i,
                    wq_hbm.at[at_rows, columns],
                    wq.at[i, pl.ds(f * width, width), :],
                )
            )
            at_heads = pl.ds(pl.multiple_of(pairs[i] * 2 * HD, 2 * HD), 2 * HD)
            columns = pl.ds(pl.multiple_of(halves[1 - f] * width, width), width)
            out_copies[i].append(local(L_OUT, wo_hbm.at[at_heads, columns], wo.at[i, f]))

    order = [CHUNKS - 1 - i for i in range(CHUNKS)]
    for p in order:
        own_copy[p].start()
    freq_copy.start()
    gain_copy.start()
    for c in kv_copies[0]:
        c.start()

    barrier = pltpu.get_barrier_semaphore()

    def greet(device):
        pl.semaphore_signal(barrier, inc=1, device_id=device, device_id_type=pl.DeviceIdType.MESH)

    greet(to_core)
    greet(to_x)
    greet(to_y)
    pl.when(has_next)(lambda: greet(to_z))
    pl.when(has_prev)(lambda: greet({"seq": me - group}))
    pl.semaphore_wait(barrier, 3 + has_next.astype(jnp.int32) + has_prev.astype(jnp.int32))

    def token_copy(p):
        return copy(S_TOKEN, TOKEN + p, own.at[chunk(p)], other.at[chunk(p)], to_core)

    for p in order:
        own_copy[p].wait()
        token_copy(p).start()
    for c in kv_copies[1]:
        c.start()
    for i in (1, 0):
        for c in q_copies[i]:
            c.start()

    def piece(ref, p):
        return ref.at[:, chunk(p), :]

    def of(r):
        return x + r - 2 * x * r

    def send_x(p):
        return copy(S_X, X_KV + p, piece(kvm, p), piece(held.at[0, x], p), to_x)

    def take_x(p):
        return copy(S_X, X_KV + p, piece(kvm, p), piece(held.at[0, 1 - x], p), to_x)

    def place(r, p):
        return r * CHUNKS + CHUNKS - 1 - p

    def move(kind, message, src, dst, b, p, device):
        return copy(kind, message, piece(held.at[src, b], p), piece(held.at[dst, b], p), device)

    def z_near(r, p):
        return move(S_Z_NEAR, Z_NEAR + place(r, p), 0, 2, of(r), p, to_z)

    def z_far(b, p):
        return move(S_Z_FAR, Z_FAR + place(1 - b, p), 2, 4, b, p, to_z)

    def z_extra(p):
        return move(S_Z_FAR, Z_EXTRA + p, 1 + 2 * y, 3 + 2 * y, 0, p, to_z)

    def y_near(src, r, p):
        return move(S_Y_NEAR, Y_NEAR + place(r, p) // (CHUNKS // UNITS), src, 1, of(r), p, to_y)

    def y_far(src, b, p):
        kind = S_Y_FAR if b == 1 else S_Y_LATE
        return move(kind, Y_FAR + place(1 - b, p) // (CHUNKS // UNITS), src, 3, b, p, to_y)

    def y_extra(p):
        return move(S_Y_EXTRA, Y_EXTRA, 3 + 2 * y, 4, 0, p, to_y)

    def rows_of(h):
        return pl.ds(pl.multiple_of(h * unit, unit), unit)

    def take_unit(message, slot, b, h):
        block = held.at[slot, b, :, rows_of(h), :]
        copy(S_Y_NEAR, message, block, block, to_y).wait_recv()

    freq_copy.wait()
    at_row = lax.broadcasted_iota(jnp.int32, (rows, LANES), 0) + me * rows
    angles = at_row.astype(jnp.float32) * freq[...]
    cosine[...] = jnp.cos(angles)
    sine[...] = jnp.sin(angles)
    gain_copy.wait()

    lines = 16
    rounds = 4
    tiles = width // LANES

    def norm_chunk(p):
        def step(i, carry):
            start = p * part + i * lines * rounds
            spots = [
                pl.ds(pl.multiple_of(start + n * lines, lines), lines) for n in range(rounds)
            ]
            scales = []
            for at in spots:
                squares = None
                for ref in (own, other):
                    for j in range(tiles):
                        value = ref[at, j * LANES : (j + 1) * LANES].astype(jnp.float32)
                        squares = value * value if squares is None else squares + value * value
                scale = lax.rsqrt(
                    jnp.sum(squares, axis=-1, keepdims=True) / (2 * width) + norm_epsilon
                )
                scales.append(jnp.broadcast_to(scale, (lines, LANES)))
            for f, ref in enumerate((own, other)):
                for j in range(tiles):
                    weight = gain[pl.ds(halves[f] * tiles + j, 1), :]
                    to = f * width + j * LANES
                    for at, scale in zip(spots, scales):
                        value = ref[at, j * LANES : (j + 1) * LANES].astype(jnp.float32)
                        normed[at, to : to + LANES] = (value * scale * weight).astype(jnp.bfloat16)
            return carry

        lax.fori_loop(0, part // (lines * rounds), step, 0)

    def project_kv(p, i, dst):
        value = jnp.dot(normed[chunk(p), :], wkv[i], preferred_element_type=jnp.float32)
        key = rotated(value[:, :HD], cosine[chunk(p), :], sine[chunk(p), :])
        dst[0, chunk(p), :] = key
        dst[1, chunk(p), :] = value[:, HD:].astype(jnp.bfloat16)

    def take_near(r, p):
        def act():
            z_near(r, p).wait_recv()
            pl.when(second_row)(lambda: y_near(2, r, p).start())

        pl.when(has_prev)(act)

    far_order = [(1, 3), (1, 2), (1, 1), (1, 0), (0, 3), (0, 2)]
    late_order = [(0, 1), (0, 0), (1, 1), (1, 0), (0, 3), (0, 2)]

    def take_far(k):
        b, p = far_order[k]

        def act():
            z_far(b, p).wait_recv()
            pl.when(second_row)(lambda: y_far(4, b, p).start())

        pl.when(has_far)(act)

    def take_extra(p):
        def act():
            z_extra(p).wait_recv()
            y_extra(p).start()

        pl.when(has_far)(act)

    def pass_extra(row):
        def act():
            for p in (1, 0):
                z_extra(p).start()

        pl.when(has_next & has_prev & (y == row))(act)

    def pass_mate(p):
        take_x(p).wait_recv()
        pl.when(has_next)(lambda: z_near(1, p).start())
        pl.when(first_row)(lambda: y_near(0, 1, p).start())

    for i, p in enumerate(order):
        token_copy(p).wait_recv()
        norm_chunk(p)
        if i == 0:
            local(L_KV, wkv.at[0], wkv.at[0]).wait()
        project_kv(p, 0, held.at[0, x])
        pl.when(has_next)(lambda: z_near(0, p).start())
        pl.when(first_row)(lambda: y_near(0, 0, p).start())
        if i == 0:
            local(L_KV + 1, wkv.at[1], wkv.at[1]).wait()
        project_kv(p, 1, kvm)
        send_x(p).start()
        if i == 0:
            for i_ in (0, 1):
                for c in out_copies[i_]:
                    c.start()
            post_copy.start()
        if i == 2:
            take_near(0, order[0])

    def project_q(i, dst):
        def step(t, carry):
            at = pl.ds(pl.multiple_of(t * unit, unit), unit)
            value = jnp.dot(normed[at, :], wq[i], preferred_element_type=jnp.float32)
            for head in range(2):
                dst[pl.ds(pl.multiple_of(head * rows + t * unit, unit), unit), :] = rotated(
                    value[:, head * HD : (head + 1) * HD], cosine[at, :], sine[at, :]
                )
            return carry

        lax.fori_loop(0, UNITS, step, 0)

    def q_copy():
        return copy(S_Q, X_Q, asked, queries.at[1], to_x)

    total[...] = jnp.zeros_like(total)
    mass[...] = jnp.zeros_like(mass)
    pass_mate(order[0])
    local(L_Q + 1, wq.at[1], wq.at[1]).wait()
    take_near(0, order[1])
    project_q(1, asked)
    q_copy().start()
    pass_mate(order[1])
    take_near(0, order[2])
    local(L_Q + 0, wq.at[0], wq.at[0]).wait()
    project_q(0, queries.at[0])
    pass_mate(order[2])
    take_near(0, order[3])
    pass_mate(order[3])

    def attend(which, slot, b, h, distance=None):
        at = pl.ds(pl.multiple_of(h * unit, unit), unit)
        scores = lax.dot_general(
            queries[which],
            held[slot, b, 0, at, :],
            (((1,), (1,)), ((), ())),
            preferred_element_type=jnp.float32,
        )
        weights = jnp.exp2(outer * jnp.tanh(scores * inner))
        if distance is not None:
            down = lax.broadcasted_iota(jnp.int32, weights.shape, 0)
            down = jnp.where(down >= rows, down - rows, down)
            offset = (distance - h * unit) + down - lax.broadcasted_iota(jnp.int32, weights.shape, 1)
            weights = jnp.where((offset >= 0) & (offset < WINDOW), weights, 0.0)
        added = None
        for k in range(unit // LANES):
            lanes = weights[:, k * LANES : (k + 1) * LANES]
            added = lanes if added is None else added + lanes
        mass[which] += added
        total[which] += jnp.dot(
            weights.astype(jnp.bfloat16), held[slot, b, 1, at, :], preferred_element_type=jnp.float32
        )

    def both(act):
        def step(s, carry):
            act(s)
            return carry

        lax.fori_loop(0, 2, step, 0)

    def attend_own(which):
        mine = of(which)

        def step(i, carry):
            b = mine - i // UNITS
            attend(which, 0, b, i % UNITS, (mine - b) * rows)
            return carry

        lax.fori_loop(0, UNITS + UNITS * mine, step, 0)

    def z_unit(u):
        return 2, of(u // UNITS), UNITS - 1 - u % UNITS

    def y_unit(w):
        return 1, of(w // UNITS), UNITS - 1 - w % UNITS

    near_there = me >= 2
    far_there = me >= 6

    def take_y(w):
        take_unit(Y_NEAR + w, *y_unit(w))

    attend_own(0)

    def near_step(u, carry):
        p = CHUNKS - 1 - u
        take_near(1, p)
        pl.when(has_prev & has_next)(lambda: z_far(1, p).start())
        pl.when(has_prev & first_row & (u < 2))(lambda: y_far(2, 1, p).start())
        pl.when(has_prev)(lambda: attend(0, *z_unit(u)))

        def with_y():
            take_y(u - 1)
            attend(0, *y_unit(u - 1))

        pl.when((u >= 1) & near_there)(with_y)
        return carry

    lax.fori_loop(0, CHUNKS, near_step, 0)

    def pass_rest():
        for p in (3, 2):
            pl.when(has_next)(lambda: z_far(0, p).start())
        for b, p in late_order:
            pl.when(first_row)(lambda: y_far(2, b, p).start())

    pl.when(has_prev)(pass_rest)

    q_copy().wait_recv()
    attend_own(1)
    take_far(0)

    def again_z(u, carry):
        attend(1, *z_unit(u))
        return carry

    def again_y(w, carry):
        attend(1, *y_unit(w))
        return carry

    def repeat(count, step):
        def act():
            lax.fori_loop(0, count, step, 0)

        return act

    pl.when(has_prev)(repeat(4, again_z))
    take_far(1)
    pl.when(near_there)(repeat(3, again_y))

    def last_near():
        take_y(3)
        both(lambda s: attend(s, *y_unit(3)))

    pl.when(near_there)(last_near)
    pass_extra(0)

    third_b = (1, 1 - y, y, 0)
    third_h = (1, 0, 1 - y, y)

    def take_third(j):
        def act():
            message = Y_FAR + 2 * (1 - third_b[j]) + 1 - third_h[j]
            take_unit(message, 3, third_b[j], third_h[j])

        pl.when(far_there & ((j < 3) | second_row))(act)

    def third(j):
        pl.when(far_there)(lambda: both(lambda s: attend(s, 3, third_b[j], third_h[j])))

    def fourth(b, h):
        def act():
            def one(s):
                mine = of(s)
                pl.when(mine <= b)(lambda: attend(s, 4, b, h, WINDOW + (mine - b) * rows))

            both(one)

        pl.when(has_far)(act)

    take_far(2)
    fourth(1, 1)
    take_third(0)
    third(0)
    take_far(3)
    fourth(1, 0)
    pl.when(second_row)(lambda: take_third(1))
    pass_extra(1)
    take_far(4)
    pl.when(first_row)(lambda: take_third(1))
    third(1)
    take_far(5)
    fourth(0, 1)
    pl.when(second_row)(lambda: take_third(2))
    pl.when(second_row)(lambda: third(2))
    take_extra(1)
    pl.when(first_row)(lambda: take_third(2))
    pl.when(first_row)(lambda: third(2))
    take_extra(0)
    take_third(3)
    pl.when(far_there)(lambda: attend(1, 3, third_b[3], third_h[3]))

    def finish(which, head, at_rows):
        at = pl.ds(head * rows + at_rows.start, at_rows.size)
        weight = jnp.sum(mass[which, at, :], axis=-1, keepdims=True)
        return (total[which, at, :] * (1.0 / weight)).astype(jnp.bfloat16)

    def out_copy(p):
        return copy(S_OUT, X_OUT + p, leaving.at[chunk(p)], landed.at[chunk(p)], to_x)

    def send_out(p):
        for head in range(2):
            leaving[chunk(p), head * HD : (head + 1) * HD] = finish(1, head, chunk(p))
        out_copy(p).start()

    def project_own(h):
        at = slice(h * unit, (h + 1) * unit)
        for p in range(h * CHUNKS // UNITS, (h + 1) * CHUNKS // UNITS):
            for head in range(2):
                finished[chunk(p), head * HD : (head + 1) * HD] = finish(0, head, chunk(p))
        for f in range(2):
            sums[f][at, :] = jnp.dot(
                finished[at, :], wo[0, f], preferred_element_type=jnp.float32
            )

    def send_low():
        send_out(1)
        send_out(0)

    send_out(3)
    send_out(2)
    pl.when(x == 0)(send_low)
    pl.when(far_there)(lambda: attend(0, 3, third_b[3], third_h[3]))
    local(L_OUT, wo, wo).wait()
    post_copy.wait()
    project_own(1)

    def last_far():
        take_unit(Y_EXTRA, 4, 0, 0)
        attend(x, 4, 0, 0, WINDOW)

    pl.when(has_far)(last_far)
    pl.when(x == 1)(send_low)
    project_own(0)

    def given_copy(p):
        return copy(S_GIVEN, GIVEN + p, given.at[chunk(p)], arrived.at[chunk(p)], to_core)

    def squares_copy(p):
        return copy(S_SQUARES, SQUARES + p, sq_own.at[chunk(p)], sq_other.at[chunk(p)], to_core)

    def add_mate(p):
        out_copy(p).wait_recv()
        theirs = landed[chunk(p), :]
        given[chunk(p), :] = (
            branch[chunk(p), :]
            + jnp.dot(theirs, wo[1, 0], preferred_element_type=jnp.float32)
        ).astype(jnp.bfloat16)
        given_copy(p).start()
        out_ref[chunk(p), :] += jnp.dot(theirs, wo[1, 1], preferred_element_type=jnp.float32)

    def groups(p):
        return [pl.ds(p * part + n * lines, lines) for n in range(part // lines)]

    columns = [slice(j * LANES, (j + 1) * LANES) for j in range(tiles)]

    def add_core(p):
        given_copy(p).wait_recv()
        for rows_at in groups(p):
            shares = [out_ref[rows_at, at] + arrived[rows_at, at].astype(jnp.float32) for at in columns]
            squares = None
            for at, share in zip(columns, shares):
                out_ref[rows_at, at] = share
                squares = share * share if squares is None else squares + share * share
            sq_own[rows_at, :] = squares
        squares_copy(p).start()

    def last(p):
        squares_copy(p).wait_recv()
        for rows_at in groups(p):
            squares = jnp.sum(sq_own[rows_at, :] + sq_other[rows_at, :], axis=-1, keepdims=True)
            scale = jnp.broadcast_to(
                lax.rsqrt(squares / (2 * width) + norm_epsilon), (lines, LANES)
            )
            values = [
                post[j : j + 1, :] * out_ref[rows_at, at] * scale for j, at in enumerate(columns)
            ]
            for at, value in zip(columns, values):
                out_ref[rows_at, at] = value

    def tail(i, carry):
        p = CHUNKS - 1 - i
        pl.when(i < CHUNKS)(lambda: add_mate(p))
        pl.when((i >= 1) & (i < CHUNKS + 1))(lambda: add_core(p + 1))
        pl.when(i >= 2)(lambda: last(p + 2))
        return carry

    lax.fori_loop(0, CHUNKS + 2, tail, 0)

    def sent(kind, ref):
        copy(kind, TOKEN, ref, ref, to_x).wait_send()

    block = held.at[0, 0]
    sent(S_TOKEN, own)
    sent(S_X, kvm)
    sent(S_Q, asked)
    sent(S_OUT, leaving)
    sent(S_GIVEN, given)
    sent(S_SQUARES, sq_own)
    pl.when(has_next)(lambda: sent(S_Z_NEAR, held.at[0]))
    pl.when(has_next & has_prev)(lambda: sent(S_Z_FAR, held.at[0]))
    pl.when(first_row | has_prev)(lambda: sent(S_Y_NEAR, held.at[0]))
    pl.when((first_row & has_prev) | has_far)(lambda: sent(S_Y_FAR, block))
    pl.when(first_row & has_prev)(lambda: sent(S_Y_LATE, block))
    pl.when(second_row & has_far)(lambda: sent(S_Y_LATE, block.at[:, rows_of(0), :]))
    pl.when(has_far)(lambda: sent(S_Y_EXTRA, block.at[:, rows_of(0), :]))


def local_layer(blocks, tokens, pre_gain, query_weight, key_weight, value_weight, out_weight, post_gain):
    rows, width = tokens.shape
    frequency = np.exp(-np.log(rope_base) * (2.0 * np.arange(HD // 2) / HD)).astype(np.float32)
    anywhere = pl.BlockSpec(memory_space=pltpu.HBM)
    bf16, f32 = jnp.bfloat16, jnp.float32
    vmem = pltpu.VMEM
    half = 2 * HD
    normed_branch = pl.pallas_call(
        functools.partial(layer_kernel, blocks),
        out_shape=vmem((rows, width), f32),
        in_specs=[anywhere] * 8,
        out_specs=pl.BlockSpec(memory_space=pltpu.VMEM),
        scratch_shapes=[
            vmem((rows, width), bf16),
            vmem((rows, width), bf16),
            vmem((2 * width // LANES, LANES), f32),
            vmem((1, LANES), f32),
            vmem((width // LANES, LANES), f32),
            vmem((rows, 2 * width), bf16),
            vmem((2, 2 * width, half), bf16),
            vmem((2, 2 * width, half), bf16),
            vmem((2, 2, half, width), bf16),
            vmem((rows, LANES), f32),
            vmem((rows, LANES), f32),
            vmem((6, 2, 2, rows, HD), bf16),
            vmem((2, rows, HD), bf16),
            vmem((2, 2 * rows, HD), bf16),
            vmem((2 * rows, HD), bf16),
            vmem((2, 2 * rows, HD), f32),
            vmem((2, 2 * rows, LANES), f32),
            vmem((rows, half), bf16),
            vmem((rows, half), bf16),
            vmem((rows, half), bf16),
            vmem((rows, width), f32),
            vmem((rows, width), bf16),
            vmem((rows, LANES), f32),
            vmem((rows, LANES), f32),
            pltpu.SemaphoreType.DMA((SENDS,)),
            pltpu.SemaphoreType.DMA((MESSAGES,)),
            pltpu.SemaphoreType.DMA((LOCALS,)),
        ],
        compiler_params=pltpu.CompilerParams(
            collective_id=0, has_side_effects=True, vmem_limit_bytes=56 * 1024 * 1024
        ),
    )(
        tokens,
        pre_gain.reshape(-1, LANES),
        jnp.asarray(frequency)[None, :],
        query_weight,
        key_weight,
        value_weight,
        out_weight,
        post_gain.reshape(-1, LANES),
    )
    return (tokens.astype(f32) + normed_branch).astype(bf16)


def solution(mesh):
    placed = (
        P("seq", "head"),
        P(),
        P(None, "head"),
        P(None, "head"),
        P(None, "head"),
        P("head", None),
        P("head"),
    )
    return jax.shard_map(
        functools.partial(local_layer, mesh.shape["seq"]),
        mesh=mesh,
        in_specs=placed,
        out_specs=P("seq", "head"),
        check_vma=False,
    )
```

time: 82.2 us -> 72.4 us (0.88)
  Pallas kernels: 79.2 us -> 70.5 us
  local copies, waits for them, and re-layouts: 2.85 us -> 0.01 us
  other arithmetic: 0 us -> 1.59 us
    pallas_call x1, Pallas kernels: 79.2 us -> 70.5 us  [local_layer(): pl.pallas_call(functools.partial(layer_kernel, blocks), out_shape=vmem((r...]
    unnamed x1 -> x2, local copies, waits for them, and re-layouts: 2.85 us -> 0.01 us
    convert_element_type x0 -> x1, other arithmetic: none -> 1.59 us  [local_layer(): return (tokens.astype(f32) + normed_branch).astype(bf16)]
where the time goes in v2:
time: 72.4 us; the launch traced here: 72.1 us
  Pallas kernels  70.5 us (97%)
  other arithmetic  1.59 us (2%)
    pallas_call x1, Pallas kernels, local_layer(): pl.pallas_call(functools.partial(layer_kernel, blocks), out_shape=vmem((r...  70.5 us
    convert_element_type x1, other arithmetic, local_layer(): return (tokens.astype(f32) + normed_branch).astype(bf16)  1.59 us

profile of v2, /device:TPU:17, one launch (start us, length us, event | category | flops | bytes accessed | tf_op | source)
XLA Modules:
  0.0 72.1 jit_solution(11907260907741294237)
XLA Ops:
  0.0 0.0 copy-start
  0.0 70.5 %shard_map.82 = f32[512,1792]{1,0:T(8,128)S(1)} custom-call(bf16[512,1792]{1,0:T(8,128)(2,1)} %tokens_hbm.1, f32[28,128]{1,0:T(8,128)} %bitcast.2, f32[1,128]{1,0:T(1,128)} %constant.3.freq_hbm, bf16[3584,1024]{1,0:T(8,128)(2,1)} %wq_hbm.1, bf16[3584,512]{1,0:T(8,128)(2,1)} %wk_hbm.1, bf16[3584,512]{1,0:T(8,128)(2,1)} %wv_hbm.1, bf16[1024,3584]{1,0:T(8,128)(2,1)} %wo_hbm.1, ...), custom_call_target="tpu_custom_call" | custom-call | tf_op jit(solution)/shard_map/pallas_call | solution.py:627
  70.5 0.0 copy-done
  70.5 1.6 %add_convert_fusion = bf16[512,1792]{1,0:T(8,128)(2,1)} fusion(f32[512,1792]{1,0:T(8,128)S(1)} %shard_map.82, bf16[512,1792]{1,0:T(8,128)(2,1)S(1)} %copy-done), kind=kLoop, calls=%fused_computation | loop fusion | flops 2752512 | bytes 7340032 | tf_op jit(solution)/shard_map/convert_element_type | solution.py:674
Async XLA Ops:
  0.0 70.5 %copy-start = (bf16[512,1792]{1,0:T(8,128)(2,1)S(1)}, bf16[512,1792]{1,0:T(8,128)(2,1)}, u32[]{:S(2)}) copy-start(bf16[512,1792]{1,0:T(8,128)(2,1)} %tokens_hbm.1) | copy-start | bytes 5505028

commit v3 on v2

--- a/solution.py
+++ b/solution.py
@@ -18,21 +18,26 @@
 norm_epsilon = 1e-06
 
 CHUNKS = 4
+
+SLABS = ((12, 4), (8, 4), (4, 4), (2, 2), (0, 2))
+OUTS = len(SLABS)
+
+STEPS = ((3, 14, 2), (3, 12, 2), (2, 8, 4), (1, 4, 4), (0, 0, 4))
 UNITS = 2
 
 TOKEN = 0
-X_KV = TOKEN + CHUNKS
+X_KV = TOKEN + len(STEPS)
 X_Q = X_KV + CHUNKS
 X_OUT = X_Q + 1
-Z_NEAR = X_OUT + CHUNKS
+Z_NEAR = X_OUT + OUTS
 Z_FAR = Z_NEAR + 2 * CHUNKS
 Z_EXTRA = Z_FAR + CHUNKS + CHUNKS // 2
 Y_NEAR = Z_EXTRA + CHUNKS // 2
 Y_FAR = Y_NEAR + 2 * UNITS
 Y_EXTRA = Y_FAR + 2 * UNITS
 GIVEN = Y_EXTRA + 1
-SQUARES = GIVEN + CHUNKS
-MESSAGES = SQUARES + CHUNKS
+SQUARES = GIVEN + OUTS
+MESSAGES = SQUARES + OUTS
 
 (
     S_TOKEN, S_X, S_Q, S_OUT, S_Z_NEAR, S_Z_FAR, S_Y_NEAR, S_Y_FAR, S_Y_LATE, S_Y_EXTRA, S_GIVEN,
@@ -40,7 +45,7 @@
 ) = range(13)
 
 L_TOKEN = 0
-L_GAIN = L_TOKEN + CHUNKS
+L_GAIN = L_TOKEN + len(STEPS)
 L_FREQ = L_GAIN + 1
 L_POST = L_FREQ + 1
 L_KV = L_POST + 1
@@ -63,7 +68,7 @@
 def layer_kernel(
     blocks, tokens_hbm, gain_hbm, freq_hbm, wq_hbm, wk_hbm, wv_hbm, wo_hbm, post_hbm, out_ref,
     own, other, gain, freq, post, normed, wkv, wq, wo, cosine, sine, held, kvm, queries, asked,
-    total, mass, leaving, landed, finished, branch, arrived, sq_own, sq_other,
+    total, mass, leaving, landed, finished, branch, kept, arrived, sq_own, sq_other,
     send_sems, recv_sems, local_sems,
 ):
     rows, width = own.shape
@@ -105,11 +110,16 @@
         return pl.ds(pl.multiple_of(p * part, part), part)
 
     given = other
-    sums = (branch, out_ref)
+    sums = (branch, kept)
     halves = (side, 1 - side)
     pairs = (x, 1 - x)
 
-    own_copy = [local(L_TOKEN + p, tokens_hbm.at[chunk(p)], own.at[chunk(p)]) for p in range(CHUNKS)]
+    steps = [
+        (p, pl.ds(first * rows // 16, size * rows // 16)) for p, first, size in STEPS
+    ]
+    own_copy = [
+        local(L_TOKEN + i, tokens_hbm.at[at], own.at[at]) for i, (_, at) in enumerate(steps)
+    ]
     gain_copy = local(L_GAIN, gain_hbm, gain)
     freq_copy = local(L_FREQ, freq_hbm, freq)
     post_copy = local(L_POST, post_hbm, post)
@@ -141,11 +151,13 @@
             out_copies[i].append(local(L_OUT, wo_hbm.at[at_heads, columns], wo.at[i, f]))
 
     order = [CHUNKS - 1 - i for i in range(CHUNKS)]
-    for p in order:
-        own_copy[p].start()
+    for c in own_copy[:2]:
+        c.start()
     freq_copy.start()
     gain_copy.start()
     for c in kv_copies[0]:
+        c.start()
+    for c in own_copy[2:]:
         c.start()
 
     barrier = pltpu.get_barrier_semaphore()
@@ -160,76 +172,84 @@
     pl.when(has_prev)(lambda: greet({"seq": me - group}))
     pl.semaphore_wait(barrier, 3 + has_next.astype(jnp.int32) + has_prev.astype(jnp.int32))
 
-    def token_copy(p):
-        return copy(S_TOKEN, TOKEN + p, own.at[chunk(p)], other.at[chunk(p)], to_core)
-
-    for p in order:
-        own_copy[p].wait()
-        token_copy(p).start()
+    def token_copy(i):
+        at = steps[i][1]
+        return copy(S_TOKEN, TOKEN + i, own.at[at], other.at[at], to_core)
+
+    for i in range(2):
+        own_copy[i].wait()
+        token_copy(i).start()
     for c in kv_copies[1]:
         c.start()
+
+    def piece(ref, p):
+        return ref.at[:, chunk(p), :]
+
+    def of(r):
+        return x + r - 2 * x * r
+
+    def send_x(p):
+        return copy(S_X, X_KV + p, piece(kvm, p), piece(held.at[0, x], p), to_x)
+
+    def take_x(p):
+        return copy(S_X, X_KV + p, piece(kvm, p), piece(held.at[0, 1 - x], p), to_x)
+
+    def place(r, p):
+        return r * CHUNKS + CHUNKS - 1 - p
+
+    def move(kind, message, src, dst, b, p, device):
+        return copy(kind, message, piece(held.at[src, b], p), piece(held.at[dst, b], p), device)
+
+    def z_near(r, p):
+        return move(S_Z_NEAR, Z_NEAR + place(r, p), 0, 2, of(r), p, to_z)
+
+    def z_far(b, p):
+        return move(S_Z_FAR, Z_FAR + place(1 - b, p), 2, 4, b, p, to_z)
+
+    def z_extra(p):
+        return move(S_Z_FAR, Z_EXTRA + p, 1 + 2 * y, 3 + 2 * y, 0, p, to_z)
+
+    def y_near(src, r, p):
+        return move(S_Y_NEAR, Y_NEAR + place(r, p) // (CHUNKS // UNITS), src, 1, of(r), p, to_y)
+
+    def y_far(src, b, p):
+        kind = S_Y_FAR if b == 1 else S_Y_LATE
+        return move(kind, Y_FAR + place(1 - b, p) // (CHUNKS // UNITS), src, 3, b, p, to_y)
+
+    def y_extra(p):
+        return move(S_Y_EXTRA, Y_EXTRA, 3 + 2 * y, 4, 0, p, to_y)
+
+    def rows_of(h):
+        return pl.ds(pl.multiple_of(h * unit, unit), unit)
+
+    def take_unit(message, slot, b, h):
+        block = held.at[slot, b, :, rows_of(h), :]
+        copy(S_Y_NEAR, message, block, block, to_y).wait_recv()
+
+    freq_copy.wait()
+
+    def turn(at):
+        at_row = lax.broadcasted_iota(jnp.int32, (at.size, LANES), 0) + (me * rows + at.start)
+        angles = at_row.astype(jnp.float32) * freq[...]
+        cosine[at, :] = jnp.cos(angles)
+        sine[at, :] = jnp.sin(angles)
+
+    turn(pl.ds(order[0] * part, part))
+    gain_copy.wait()
+    for i in range(2, len(steps)):
+        own_copy[i].wait()
+        token_copy(i).start()
     for i in (1, 0):
         for c in q_copies[i]:
             c.start()
 
-    def piece(ref, p):
-        return ref.at[:, chunk(p), :]
-
-    def of(r):
-        return x + r - 2 * x * r
-
-    def send_x(p):
-        return copy(S_X, X_KV + p, piece(kvm, p), piece(held.at[0, x], p), to_x)
-
-    def take_x(p):
-        return copy(S_X, X_KV + p, piece(kvm, p), piece(held.at[0, 1 - x], p), to_x)
-
-    def place(r, p):
-        return r * CHUNKS + CHUNKS - 1 - p
-
-    def move(kind, message, src, dst, b, p, device):
-        return copy(kind, message, piece(held.at[src, b], p), piece(held.at[dst, b], p), device)
-
-    def z_near(r, p):
-        return move(S_Z_NEAR, Z_NEAR + place(r, p), 0, 2, of(r), p, to_z)
-
-    def z_far(b, p):
-        return move(S_Z_FAR, Z_FAR + place(1 - b, p), 2, 4, b, p, to_z)
-
-    def z_extra(p):
-        return move(S_Z_FAR, Z_EXTRA + p, 1 + 2 * y, 3 + 2 * y, 0, p, to_z)
-
-    def y_near(src, r, p):
-        return move(S_Y_NEAR, Y_NEAR + place(r, p) // (CHUNKS // UNITS), src, 1, of(r), p, to_y)
-
-    def y_far(src, b, p):
-        kind = S_Y_FAR if b == 1 else S_Y_LATE
-        return move(kind, Y_FAR + place(1 - b, p) // (CHUNKS // UNITS), src, 3, b, p, to_y)
-
-    def y_extra(p):
-        return move(S_Y_EXTRA, Y_EXTRA, 3 + 2 * y, 4, 0, p, to_y)
-
-    def rows_of(h):
-        return pl.ds(pl.multiple_of(h * unit, unit), unit)
-
-    def take_unit(message, slot, b, h):
-        block = held.at[slot, b, :, rows_of(h), :]
-        copy(S_Y_NEAR, message, block, block, to_y).wait_recv()
-
-    freq_copy.wait()
-    at_row = lax.broadcasted_iota(jnp.int32, (rows, LANES), 0) + me * rows
-    angles = at_row.astype(jnp.float32) * freq[...]
-    cosine[...] = jnp.cos(angles)
-    sine[...] = jnp.sin(angles)
-    gain_copy.wait()
-
     lines = 16
     rounds = 4
     tiles = width // LANES
 
-    def norm_chunk(p):
+    def norm_chunk(rows_at):
         def step(i, carry):
-            start = p * part + i * lines * rounds
+            start = rows_at.start + i * lines * rounds
             spots = [
                 pl.ds(pl.multiple_of(start + n * lines, lines), lines) for n in range(rounds)
             ]
@@ -253,13 +273,13 @@
                         normed[at, to : to + LANES] = (value * scale * weight).astype(jnp.bfloat16)
             return carry
 
-        lax.fori_loop(0, part // (lines * rounds), step, 0)
-
-    def project_kv(p, i, dst):
-        value = jnp.dot(normed[chunk(p), :], wkv[i], preferred_element_type=jnp.float32)
-        key = rotated(value[:, :HD], cosine[chunk(p), :], sine[chunk(p), :])
-        dst[0, chunk(p), :] = key
-        dst[1, chunk(p), :] = value[:, HD:].astype(jnp.bfloat16)
+        lax.fori_loop(0, rows_at.size // (lines * rounds), step, 0)
+
+    def project_kv(at, i, dst):
+        value = jnp.dot(normed[at, :], wkv[i], preferred_element_type=jnp.float32)
+        key = rotated(value[:, :HD], cosine[at, :], sine[at, :])
+        dst[0, at, :] = key
+        dst[1, at, :] = value[:, HD:].astype(jnp.bfloat16)
 
     def take_near(r, p):
         def act():
@@ -299,23 +319,36 @@
         pl.when(has_next)(lambda: z_near(1, p).start())
         pl.when(first_row)(lambda: y_near(0, 1, p).start())
 
-    for i, p in enumerate(order):
-        token_copy(p).wait_recv()
-        norm_chunk(p)
+    def rows_copy(kind, message, src, dst, at, device):
+        copy(kind, message, src.at[:, at, :], dst.at[:, at, :], device).start()
+
+    for i, (p, at) in enumerate(steps):
+        token_copy(i).wait_recv()
+        norm_chunk(at)
+        if i > 1:
+            turn(at)
         if i == 0:
             local(L_KV, wkv.at[0], wkv.at[0]).wait()
-        project_kv(p, 0, held.at[0, x])
-        pl.when(has_next)(lambda: z_near(0, p).start())
-        pl.when(first_row)(lambda: y_near(0, 0, p).start())
+        project_kv(at, 0, held.at[0, x])
+
+        def near_rows(slot, kind, message, device):
+            rows_copy(kind, message, held.at[0, x], held.at[slot, x], at, device)
+
+        pl.when(has_next)(lambda: near_rows(2, S_Z_NEAR, Z_NEAR + place(0, p), to_z))
+        pl.when(first_row)(
+            lambda: near_rows(1, S_Y_NEAR, Y_NEAR + place(0, p) // (CHUNKS // UNITS), to_y)
+        )
         if i == 0:
+            continue
+        if i == 4:
+            take_near(0, order[1])
+        if i == 1:
             local(L_KV + 1, wkv.at[1], wkv.at[1]).wait()
-        project_kv(p, 1, kvm)
+            for c in out_copies[0] + out_copies[1]:
+                c.start()
+            post_copy.start()
+        project_kv(pl.ds(p * part, part), 1, kvm)
         send_x(p).start()
-        if i == 0:
-            for i_ in (0, 1):
-                for c in out_copies[i_]:
-                    c.start()
-            post_copy.start()
         if i == 2:
             take_near(0, order[0])
 
@@ -338,7 +371,6 @@
     mass[...] = jnp.zeros_like(mass)
     pass_mate(order[0])
     local(L_Q + 1, wq.at[1], wq.at[1]).wait()
-    take_near(0, order[1])
     project_q(1, asked)
     q_copy().start()
     pass_mate(order[1])
@@ -384,6 +416,8 @@
 
         def step(i, carry):
             b = mine - i // UNITS
+            if which == 1:
+                pl.when(i == 1)(lambda: take_far(0))
             attend(which, 0, b, i % UNITS, (mine - b) * rows)
             return carry
 
@@ -401,13 +435,17 @@
     def take_y(w):
         take_unit(Y_NEAR + w, *y_unit(w))
 
-    attend_own(0)
-
-    def near_step(u, carry):
+    def near_pass(u):
         p = CHUNKS - 1 - u
         take_near(1, p)
         pl.when(has_prev & has_next)(lambda: z_far(1, p).start())
         pl.when(has_prev & first_row & (u < 2))(lambda: y_far(2, 1, p).start())
+
+    near_pass(0)
+    attend_own(0)
+
+    def near_step(u, carry):
+        pl.when(u >= 1)(lambda: near_pass(u))
         pl.when(has_prev)(lambda: attend(0, *z_unit(u)))
 
         def with_y():
@@ -429,13 +467,14 @@
 
     q_copy().wait_recv()
     attend_own(1)
-    take_far(0)
 
     def again_z(u, carry):
+        pl.when(u == 1)(lambda: take_far(1))
         attend(1, *z_unit(u))
         return carry
 
     def again_y(w, carry):
+        pl.when(w == 2)(lambda: take_far(2))
         attend(1, *y_unit(w))
         return carry
 
@@ -446,7 +485,6 @@
         return act
 
     pl.when(has_prev)(repeat(4, again_z))
-    take_far(1)
     pl.when(near_there)(repeat(3, again_y))
 
     def last_near():
@@ -479,15 +517,14 @@
 
         pl.when(has_far)(act)
 
-    take_far(2)
+    take_far(3)
     fourth(1, 1)
     take_third(0)
     third(0)
-    take_far(3)
+    take_far(4)
     fourth(1, 0)
     pl.when(second_row)(lambda: take_third(1))
     pass_extra(1)
-    take_far(4)
     pl.when(first_row)(lambda: take_third(1))
     third(1)
     take_far(5)
@@ -496,10 +533,18 @@
     pl.when(second_row)(lambda: third(2))
     take_extra(1)
     pl.when(first_row)(lambda: take_third(2))
-    pl.when(first_row)(lambda: third(2))
+
+    def late(which):
+        attend(which, 3, third_b[2], third_h[2])
+
+    pl.when(far_there & first_row)(lambda: late(1))
     take_extra(0)
     take_third(3)
     pl.when(far_there)(lambda: attend(1, 3, third_b[3], third_h[3]))
+
+    def slab(p):
+        first, size = SLABS[p]
+        return pl.ds(first * rows // 16, size * rows // 16)
 
     def finish(which, head, at_rows):
         at = pl.ds(head * rows + at_rows.start, at_rows.size)
@@ -507,30 +552,34 @@
         return (total[which, at, :] * (1.0 / weight)).astype(jnp.bfloat16)
 
     def out_copy(p):
-        return copy(S_OUT, X_OUT + p, leaving.at[chunk(p)], landed.at[chunk(p)], to_x)
+        return copy(S_OUT, X_OUT + p, leaving.at[slab(p)], landed.at[slab(p)], to_x)
 
     def send_out(p):
         for head in range(2):
-            leaving[chunk(p), head * HD : (head + 1) * HD] = finish(1, head, chunk(p))
+            leaving[slab(p), head * HD : (head + 1) * HD] = finish(1, head, slab(p))
         out_copy(p).start()
 
     def project_own(h):
         at = slice(h * unit, (h + 1) * unit)
-        for p in range(h * CHUNKS // UNITS, (h + 1) * CHUNKS // UNITS):
+        for p in (range(2) if h else range(2, OUTS)):
             for head in range(2):
-                finished[chunk(p), head * HD : (head + 1) * HD] = finish(0, head, chunk(p))
+                finished[slab(p), head * HD : (head + 1) * HD] = finish(0, head, slab(p))
         for f in range(2):
             sums[f][at, :] = jnp.dot(
                 finished[at, :], wo[0, f], preferred_element_type=jnp.float32
             )
 
     def send_low():
-        send_out(1)
-        send_out(0)
-
-    send_out(3)
-    send_out(2)
+        for p in range(2, OUTS):
+            send_out(p)
+
+    def send_high():
+        for p in range(2):
+            send_out(p)
+
+    send_high()
     pl.when(x == 0)(send_low)
+    pl.when(far_there & first_row)(lambda: late(0))
     pl.when(far_there)(lambda: attend(0, 3, third_b[3], third_h[3]))
     local(L_OUT, wo, wo).wait()
     post_copy.wait()
@@ -545,33 +594,36 @@
     project_own(0)
 
     def given_copy(p):
-        return copy(S_GIVEN, GIVEN + p, given.at[chunk(p)], arrived.at[chunk(p)], to_core)
+        return copy(S_GIVEN, GIVEN + p, given.at[slab(p)], arrived.at[slab(p)], to_core)
 
     def squares_copy(p):
-        return copy(S_SQUARES, SQUARES + p, sq_own.at[chunk(p)], sq_other.at[chunk(p)], to_core)
-
-    def add_mate(p):
+        return copy(S_SQUARES, SQUARES + p, sq_own.at[slab(p)], sq_other.at[slab(p)], to_core)
+
+    def give(p):
         out_copy(p).wait_recv()
-        theirs = landed[chunk(p), :]
-        given[chunk(p), :] = (
-            branch[chunk(p), :]
-            + jnp.dot(theirs, wo[1, 0], preferred_element_type=jnp.float32)
+        given[slab(p), :] = (
+            branch[slab(p), :]
+            + jnp.dot(landed[slab(p), :], wo[1, 0], preferred_element_type=jnp.float32)
         ).astype(jnp.bfloat16)
         given_copy(p).start()
-        out_ref[chunk(p), :] += jnp.dot(theirs, wo[1, 1], preferred_element_type=jnp.float32)
+
+    def keep(p):
+        kept[slab(p), :] += jnp.dot(
+            landed[slab(p), :], wo[1, 1], preferred_element_type=jnp.float32
+        )
 
     def groups(p):
-        return [pl.ds(p * part + n * lines, lines) for n in range(part // lines)]
+        return [pl.ds(slab(p).start + n * lines, lines) for n in range(slab(p).size // lines)]
 
     columns = [slice(j * LANES, (j + 1) * LANES) for j in range(tiles)]
 
     def add_core(p):
         given_copy(p).wait_recv()
         for rows_at in groups(p):
-            shares = [out_ref[rows_at, at] + arrived[rows_at, at].astype(jnp.float32) for at in columns]
+            shares = [kept[rows_at, at] + arrived[rows_at, at].astype(jnp.float32) for at in columns]
             squares = None
             for at, share in zip(columns, shares):
-                out_ref[rows_at, at] = share
+                kept[rows_at, at] = share
                 squares = share * share if squares is None else squares + share * share
             sq_own[rows_at, :] = squares
         squares_copy(p).start()
@@ -584,19 +636,30 @@
                 lax.rsqrt(squares / (2 * width) + norm_epsilon), (lines, LANES)
             )
             values = [
-                post[j : j + 1, :] * out_ref[rows_at, at] * scale for j, at in enumerate(columns)
+                own[rows_at, at].astype(jnp.float32) + post[j : j + 1, :] * kept[rows_at, at] * scale
+                for j, at in enumerate(columns)
             ]
             for at, value in zip(columns, values):
-                out_ref[rows_at, at] = value
-
-    def tail(i, carry):
-        p = CHUNKS - 1 - i
-        pl.when(i < CHUNKS)(lambda: add_mate(p))
-        pl.when((i >= 1) & (i < CHUNKS + 1))(lambda: add_core(p + 1))
-        pl.when(i >= 2)(lambda: last(p + 2))
-        return carry
-
-    lax.fori_loop(0, CHUNKS + 2, tail, 0)
+                out_ref[rows_at, at] = value.astype(jnp.bfloat16)
+
+    for p in range(OUTS - 2):
+        give(p)
+        keep(p)
+        if p >= 1:
+            add_core(p - 1)
+        if p >= 2:
+            last(p - 2)
+    give(OUTS - 2)
+    add_core(OUTS - 3)
+    last(OUTS - 4)
+    give(OUTS - 1)
+    keep(OUTS - 2)
+    keep(OUTS - 1)
+    last(OUTS - 3)
+    add_core(OUTS - 2)
+    add_core(OUTS - 1)
+    last(OUTS - 2)
+    last(OUTS - 1)
 
     def sent(kind, ref):
         copy(kind, TOKEN, ref, ref, to_x).wait_send()
@@ -626,7 +689,7 @@
     half = 2 * HD
     normed_branch = pl.pallas_call(
         functools.partial(layer_kernel, blocks),
-        out_shape=vmem((rows, width), f32),
+        out_shape=vmem((rows, width), bf16),
         in_specs=[anywhere] * 8,
         out_specs=pl.BlockSpec(memory_space=pltpu.VMEM),
         scratch_shapes=[
@@ -651,6 +714,7 @@
             vmem((rows, half), bf16),
             vmem((rows, half), bf16),
             vmem((rows, width), f32),
+            vmem((rows, width), f32),
             vmem((rows, width), bf16),
             vmem((rows, LANES), f32),
             vmem((rows, LANES), f32),
@@ -659,7 +723,7 @@
             pltpu.SemaphoreType.DMA((LOCALS,)),
         ],
         compiler_params=pltpu.CompilerParams(
-            collective_id=0, has_side_effects=True, vmem_limit_bytes=56 * 1024 * 1024
+            collective_id=0, has_side_effects=True, vmem_limit_bytes=58 * 1024 * 1024
         ),
     )(
         tokens,
@@ -671,7 +735,7 @@
         out_weight,
         post_gain.reshape(-1, LANES),
     )
-    return (tokens.astype(f32) + normed_branch).astype(bf16)
+    return normed_branch
 
 
 def solution(mesh):

time: 72.4 us -> 70.5 us (0.974)
  other arithmetic: 1.59 us -> 0 us
  Pallas kernels: 70.5 us -> 69 us
  local copies, waits for them, and re-layouts: 0.01 us -> 1.23 us
    convert_element_type x1 -> x0, other arithmetic: 1.59 us -> none  [local_layer(): return (tokens.astype(f32) + normed_branch).astype(bf16)]
    pallas_call x1, Pallas kernels: 70.5 us -> 69 us  [local_layer(): pl.pallas_call(functools.partial(layer_kernel, blocks), out_shape=vmem((r...]
    unnamed x2 -> x1, local copies, waits for them, and re-layouts: 0.01 us -> 1.23 us
where the time goes in v3:
time: 70.5 us; the launch traced here: 70.2 us
  Pallas kernels  69 us (98%)
  local copies, waits for them, and re-layouts  1.23 us (2%)
    pallas_call x1, Pallas kernels, local_layer(): pl.pallas_call(functools.partial(layer_kernel, blocks), out_shape=vmem((r...  69 us

profile of v3, /device:TPU:17, one launch (start us, length us, event | category | flops | bytes accessed | tf_op | source)
XLA Modules:
  0.0 70.2 jit_solution(14790172069071364916)
XLA Ops:
  0.0 69.0 %shard_map.82 = bf16[512,1792]{1,0:T(8,128)(2,1)S(1)} custom-call(bf16[512,1792]{1,0:T(8,128)(2,1)} %tokens_hbm.1, f32[28,128]{1,0:T(8,128)} %bitcast.2, f32[1,128]{1,0:T(1,128)} %constant.3.freq_hbm, bf16[3584,1024]{1,0:T(8,128)(2,1)} %wq_hbm.1, bf16[3584,512]{1,0:T(8,128)(2,1)} %wk_hbm.1, bf16[3584,512]{1,0:T(8,128)(2,1)} %wv_hbm.1, ...), custom_call_target="tpu_custom_call" | custom-call | tf_op jit(solution)/shard_map/pallas_call | solution.py:690
  69.0 1.2 %copy.10 = bf16[512,1792]{1,0:T(8,128)(2,1)} copy(bf16[512,1792]{1,0:T(8,128)(2,1)S(1)} %shard_map.82) | data formatting | bytes 3670016

commit v4 on v3

--- a/solution.py
+++ b/solution.py
@@ -650,16 +650,13 @@
         if p >= 2:
             last(p - 2)
     give(OUTS - 2)
-    add_core(OUTS - 3)
-    last(OUTS - 4)
     give(OUTS - 1)
     keep(OUTS - 2)
     keep(OUTS - 1)
-    last(OUTS - 3)
-    add_core(OUTS - 2)
-    add_core(OUTS - 1)
-    last(OUTS - 2)
-    last(OUTS - 1)
+    for p in range(OUTS - 3, OUTS):
+        add_core(p)
+    for p in range(OUTS - 4, OUTS):
+        last(p)
 
     def sent(kind, ref):
         copy(kind, TOKEN, ref, ref, to_x).wait_send()

time: 70.5 us -> 70 us (level)
  no operation moved by 1% of the time
where the time goes in v4:
time: 70 us; the launch traced here: 69.9 us
  Pallas kernels  68.6 us (98%)
  local copies, waits for them, and re-layouts  1.23 us (2%)
    pallas_call x1, Pallas kernels, local_layer(): pl.pallas_call(functools.partial(layer_kernel, blocks), out_shape=vmem((r...  68.6 us

profile of v4, /device:TPU:17, one launch (start us, length us, event | category | flops | bytes accessed | tf_op | source)
XLA Modules:
  0.0 69.9 jit_solution(14137252761273781329)
XLA Ops:
  0.0 68.6 %shard_map.82 = bf16[512,1792]{1,0:T(8,128)(2,1)S(1)} custom-call(bf16[512,1792]{1,0:T(8,128)(2,1)} %tokens_hbm.1, f32[28,128]{1,0:T(8,128)} %bitcast.2, f32[1,128]{1,0:T(1,128)} %constant.3.freq_hbm, bf16[3584,1024]{1,0:T(8,128)(2,1)} %wq_hbm.1, bf16[3584,512]{1,0:T(8,128)(2,1)} %wk_hbm.1, bf16[3584,512]{1,0:T(8,128)(2,1)} %wv_hbm.1, ...), custom_call_target="tpu_custom_call" | custom-call | tf_op jit(solution)/shard_map/pallas_call | solution.py:687
  68.6 1.2 %copy.10 = bf16[512,1792]{1,0:T(8,128)(2,1)} copy(bf16[512,1792]{1,0:T(8,128)(2,1)S(1)} %shard_map.82) | data formatting | bytes 3670016
